TPU v7x, 128 devices: a whole 4x4x4 slice. The times are simulated.
128 devices in a mesh: row: 8 (over z_lo, y), col: 16 (over x, z_hi, core).
Axes of the slice: x: 4, y: 4, z: 4 (z_hi: 2, z_lo: 2; z = z_hi * 2 + z_lo), core: 2. Of those that a mesh axis runs over, the one named last changes fastest.
Arguments:
- panel: bfloat16 [524288, 256], P(('row', 'col')), may hold values from -6 to 6
- row_basis: bfloat16 [524288, 16], P('row'), may hold values from -1.5 to 1.5
- col_basis: bfloat16 [524288, 16], P(('row', 'col')), may hold values from -0.375 to 0.375
- near_blocks: bfloat16 [2048, 9, 256, 256], P(('row', 'col')), may hold values from -0.125 to 0.125
- couplings: bfloat16 [8, 16, 512, 16, 16], P('row', 'col'), may hold values from -0.375 to 0.375
- blk_rows: int32 [8, 16, 512], P('row', 'col'), may hold values from 0 to 255
- blk_cols: int32 [8, 16, 512], P('row', 'col'), may hold values from 0 to 127
- blk_count: int32 [8, 16], P('row', 'col'), may hold values from 64 to 512, as said below
Outputs:
- product: bfloat16 [524288, 256], P(('row', 'col'))
Inputs may be any that keep to these rules, and one draw needn't show every extreme that they name: `blk_count`: slots at or past a device's count hold in-range indices and are not part of the matrix; in every draw some device holds 512 live slots.
All inputs are finite; a program needn't handle non-finite values.
Results may differ from a plain program's by a relative error of at most 0.0052.
Values may be sent and summed in bfloat16 or wider, within the bound.
No kernel may reach another device: no remote copies, remote signals or barrier semaphores. Data moves between devices by JAX's collectives and lax.ppermute only.
A program may use at most 192 MiB of HBM per device.

v0:
```python
import jax
import jax.numpy as jnp
from jax import lax
from jax.sharding import PartitionSpec as P


def padded_2(array, sides, width):
    edges = {}
    for axis, dim in sides:
        peers, length = (lax.axis_size(axis), array.shape[dim])
        up = [(i, (i + 1) % peers) for i in range(peers - 1)]
        last = lax.slice_in_dim(array, length - width, length, axis=dim)
        leading = lax.slice_in_dim(array, 0, width, axis=dim)
        edges[dim] = (
            lax.ppermute(last, axis, up),
            lax.ppermute(leading, axis, [(b, a) for a, b in up]),
        )
    done = []
    for _, dim in sides:
        low, high = edges[dim]
        around = [(width, width) if d in done else (0, 0) for d in range(array.ndim)]
        array = jnp.concatenate([jnp.pad(low, around), array, jnp.pad(high, around)], axis=dim)
        done.append(dim)
    return array


def laid_out(parts, dim):
    lengths = list(parts.shape[1:])
    lengths[dim] *= parts.shape[0]
    return jnp.moveaxis(parts, 0, dim).reshape(lengths)


def copy_for_each(array, axis):
    peers = lax.axis_size(axis)
    return lax.all_to_all(
        jnp.broadcast_to(array[None], (peers, *array.shape)), axis, 0, 0, tiled=True
    )


def gather_directly(array, axis, dim):
    return laid_out(copy_for_each(array, axis), dim)


def cut_along(array, dim, peers):
    before, after = (array.shape[:dim], array.shape[dim + 1 :])
    return jnp.moveaxis(array.reshape(*before, peers, -1, *after), dim, 0)


def sent_and_summed(array, axis, dim):
    parts = cut_along(array, dim, lax.axis_size(axis))
    arrived = lax.all_to_all(parts, axis, split_axis=0, concat_axis=0, tiled=True)
    return arrived.astype(jnp.float32).sum(axis=0)


def near_part(panel, near_blocks):
    own_rows, panel_cols = panel.shape
    leaf_size = near_blocks.shape[2]
    near_count = near_blocks.shape[1]
    half_band = near_count // 2
    cluster_dev = own_rows // leaf_size
    padded = padded_2(panel, ((("row", "col"), 0),), half_band * leaf_size)
    windows = padded.reshape(cluster_dev + 2 * half_band, leaf_size, panel_cols)
    stacked = jnp.stack(
        [windows[offset : offset + cluster_dev] for offset in range(near_count)], axis=1
    )
    result = jnp.einsum("kopq,koqn->kpn", near_blocks, stacked, preferred_element_type=jnp.float32)
    return result.reshape(own_rows, panel_cols)


def far_part(panel, row_basis, col_basis, couplings, blk_rows, blk_cols, blk_count, leaf_size):
    own_rows, panel_cols = panel.shape
    rank_size = col_basis.shape[1]
    cluster_dev = own_rows // leaf_size
    coeffs = jnp.einsum(
        "kpr,kpn->krn",
        col_basis.reshape(cluster_dev, leaf_size, rank_size),
        panel.reshape(cluster_dev, leaf_size, panel_cols),
        preferred_element_type=jnp.float32,
    ).astype(jnp.bfloat16)
    gathered = gather_directly(coeffs, "row", 0)
    slots = couplings.shape[2]
    picked = gathered[blk_cols.reshape(slots)]
    block_terms = jnp.einsum(
        "bij,bjn->bin",
        couplings.reshape(slots, rank_size, rank_size),
        picked,
        preferred_element_type=jnp.float32,
    )
    group_clusters = lax.axis_size("col") * cluster_dev
    is_live = jnp.arange(slots, dtype=jnp.int32) < blk_count.reshape(())
    one_hot = (
        (blk_rows.reshape(slots)[None, :] == jnp.arange(group_clusters, dtype=jnp.int32)[:, None])
        & is_live[None, :]
    ).astype(jnp.float32)
    partial_value = jnp.dot(
        one_hot, block_terms.reshape(slots, rank_size * panel_cols), precision=lax.Precision.HIGHEST
    )
    partial_value = partial_value.reshape(group_clusters, rank_size, panel_cols)
    coupled = sent_and_summed(partial_value.astype(jnp.bfloat16), "col", 0)
    own_basis = lax.dynamic_slice_in_dim(row_basis, lax.axis_index("col") * own_rows, own_rows, 0)
    own_basis = own_basis.reshape(cluster_dev, leaf_size, rank_size).astype(jnp.float32)
    return jnp.einsum("kpr,krn->kpn", own_basis, coupled, precision=lax.Precision.HIGHEST).reshape(
        own_rows, panel_cols
    )


def on_device(panel, row_basis, col_basis, near_blocks, couplings, blk_rows, blk_cols, blk_count):
    leaf_size = near_blocks.shape[2]
    far_field = far_part(
        panel, row_basis, col_basis, couplings, blk_rows, blk_cols, blk_count, leaf_size
    )
    near_field = near_part(panel, near_blocks)
    return (near_field + far_field).astype(jnp.bfloat16)


def solution(mesh):
    placed = (
        P(("row", "col"), None),
        P("row", None),
        P(("row", "col"), None),
        P(("row", "col"), None, None, None),
        P("row", "col", None, None, None),
        P("row", "col", None),
        P("row", "col", None),
        P("row", "col"),
    )
    return jax.shard_map(
        on_device, mesh=mesh, in_specs=placed, out_specs=P(("row", "col"), None), check_vma=False
    )
```

profile of v0, /device:TPU:16, one launch (start us, length us, event | category | flops | bytes accessed | tf_op | source)
XLA Modules:
  0.0 141.0 jit_solution(13548000087172162547)
XLA Ops:
  0.0 0.0 copy-start
  0.0 2.5 %fusion.14 = (bf16[1024,256]{1,0:T(8,128)(2,1)}, bf16[1024,256]{1,0:T(8,128)(2,1)}) fusion(bf16[4096,256]{1,0:T(8,128)(2,1)} %param.8), kind=kLoop, calls=%fused_computation.36 | loop fusion | bytes 2097152 | tf_op jit(solution)/shard_map/slice | solution.py:13
  2.5 1.9 %collective-permute-start = (bf16[1024,256]{1,0:T(8,128)(2,1)}, bf16[1024,256]{1,0:T(8,128)(2,1)S(1)}, u32[]{:S(2)}, u32[]{:S(2)}) collective-permute-start(bf16[1024,256]{1,0:T(8,128)(2,1)} %get-tuple-element.14), channel_id=1, source_target_pairs={{0,1},{1,2},{2,3},{3,4},{4,5},{5,6},{6,7},{7,8},{8,9},{9,10},{10,1... | collective-permute-start | bytes 1572872 | tf_op jit(solution)/shard_map/ppermute | solution.py:15
  4.4 8.2 %collective-permute-start.1 = (bf16[1024,256]{1,0:T(8,128)(2,1)}, bf16[1024,256]{1,0:T(8,128)(2,1)S(1)}, u32[]{:S(2)}, u32[]{:S(2)}) collective-permute-start(bf16[1024,256]{1,0:T(8,128)(2,1)} %get-tuple-element.13), channel_id=1, source_target_pairs={{1,0},{2,1},{3,2},{4,3},{5,4},{6,5},{7,6},{8,7},{9,8},{10,9},{11,1... | collective-permute-start | bytes 1572872 | tf_op jit(solution)/shard_map/ppermute | solution.py:16
  12.5 0.0 copy-start.4
  12.6 0.0 copy-start.2
  12.6 2.1 %convolution_convert_fusion.1 = bf16[16,16,256]{2,1,0:T(8,128)(2,1)S(1)} fusion(bf16[16,256,256]{2,1,0:T(8,128)(2,1)} %bitcast.53, bf16[2,16,8,256]{3,2,1,0:T(8,128)(2,1)} %bitcast.66), kind=kOutput, calls=%fused_computation.5 | convolution fusion | flops 33619968 | bytes 2359296 | tf_op jit(solution)/shard_map/kpr,kpn->krn/dot_general | solution.py:74
  14.7 1.1 broadcast_in_dim.2
  15.7 6.2 %all-to-all-start = ((bf16[8,16,16,256]{3,2,1,0:T(8,128)(2,1)}), bf16[8,16,16,256]{3,2,1,0:T(8,128)(2,1)}, u32[]{:S(2)}, u32[]{:S(2)}) async-start(bf16[8,16,16,256]{3,2,1,0:T(8,128)(2,1)} %broadcast_in_dim.2), calls=%async_computation | async-start | bytes 2097152 | tf_op jit(solution)/shard_map/all_to_all | solution.py:35
  21.9 0.0 copy-done.4
  21.9 0.0 copy-done.2
  21.9 2.8 %copy.17 = bf16[512,16,16]{2,1,0:T(8,128)(2,1)} copy(bf16[512,16,16]{0,2,1:T(8,128)(2,1)S(1)} %bitcast.65) | data formatting | bytes 524288 | tf_op jit(solution)/shard_map/reshape | solution.py:85
  25.4 0.0 copy-done
  25.4 0.0 collective-permute-done
  25.5 1.9 %constant_dynamic-update-slice_fusion.3 = (bf16[5120,256]{1,0:T(8,128)(2,1)S(1)}, bf16[5120,256]{1,0:T(8,128)(2,1)S(1)}) fusion(bf16[4096,256]{1,0:T(8,128)(2,1)} %param.8, bf16[5120,256]{1,0:T(8,128)(2,1)S(1)} %constant_dynamic-update-slice_fusion.1), kind=kLoop, calls=%fused_computation.20 | loop fusion | bytes 6291456
  27.3 0.6 fusion.13
  27.9 1.5 %constant_dynamic-update-slice_fusion.12 = bf16[16,9,256,256]{3,2,1,0:T(8,128)(2,1)} fusion(bf16[16,1,256,256]{3,2,1,0:T(8,128)(2,1)S(1)} %bitcast.63), kind=kLoop, calls=%fused_computation.29 | loop fusion | bytes 4194304
  29.5 1.5 %constant_dynamic-update-slice_fusion.11 = bf16[16,9,256,256]{3,2,1,0:T(8,128)(2,1)} fusion(bf16[16,9,256,256]{3,2,1,0:T(8,128)(2,1)} %constant_dynamic-update-slice_fusion.12, bf16[16,1,256,256]{3,2,1,0:T(8,128)(2,1)S(1)} %bitcast.61), kind=kLoop, calls=%fused_computation.28 | loop fusion | bytes 4194304
  31.0 1.5 %constant_dynamic-update-slice_fusion.10 = bf16[16,9,256,256]{3,2,1,0:T(8,128)(2,1)} fusion(bf16[16,9,256,256]{3,2,1,0:T(8,128)(2,1)} %constant_dynamic-update-slice_fusion.11, bf16[16,1,256,256]{3,2,1,0:T(8,128)(2,1)S(1)} %bitcast.59), kind=kLoop, calls=%fused_computation.27 | loop fusion | bytes 4194304
  32.5 1.6 %constant_dynamic-update-slice_fusion.9 = bf16[16,9,256,256]{3,2,1,0:T(8,128)(2,1)} fusion(bf16[16,9,256,256]{3,2,1,0:T(8,128)(2,1)} %constant_dynamic-update-slice_fusion.10, bf16[16,1,256,256]{3,2,1,0:T(8,128)(2,1)S(1)} %bitcast.57), kind=kLoop, calls=%fused_computation.26 | loop fusion | bytes 4194304
  34.1 0.0 all-to-all-done
  34.1 4.2 %gather_fusion = bf16[512,16,256]{2,1,0:T(8,128)(2,1)} fusion(bf16[128,16,256]{2,1,0:T(8,128)(2,1)} %bitcast.16, s32[1024]{0:T(1024)S(1)} %pad_clamp_fusion), kind=kCustom, calls=%fused_computation | custom fusion | bytes 8390656 | tf_op jit(solution)/shard_map/gather | solution.py:82
  38.3 4.0 %fusion.15 = f32[512,256,16]{1,2,0:T(8,128)S(1)} fusion(bf16[512,16,16]{2,1,0:T(8,128)(2,1)} %copy.17, bf16[512,16,256]{2,1,0:T(8,128)(2,1)} %gather_fusion), kind=kOutput, calls=%fused_computation.37 | convolution fusion | flops 67108864 | bytes 12845056 | tf_op jit(solution)/shard_map/bij,bjn->bin/dot_general | solution.py:83
  42.3 11.5 %copy.27 = f32[64,8,16,256]{3,1,2,0:T(8,128)} copy(f32[64,8,16,256]{3,2,1,0:T(8,128)S(1)} %bitcast.50) | data formatting | bytes 16777216
  53.8 0.0 copy-start.3
  53.8 9.0 %copy.18 = f32[4096,512]{1,0:T(8,128)} copy(f32[4096,512]{0,1:T(8,128)} %bitcast.52) | data formatting | bytes 16777216 | tf_op jit(solution)/shard_map/dot_general | solution.py:95
  62.9 0.0 copy-done.3
  62.9 12.9 %convolution_convert_fusion = bf16[256,16,256]{2,0,1:T(8,128)(2,1)S(1)} fusion(f32[16,256,512]{2,1,0:T(8,128)} %bitcast.51, s32[512]{0:T(512)S(1)} %bitcast.68, pred[512]{0:T(512)(128)(4,1)S(1)} %iota_compare_fusion.1), kind=kOutput, calls=%fused_computation.4 | convolution fusion | flops 6443761664 | bytes 10488320 | tf_op jit(solution)/shard_map/dot_general | solution.py:95
  75.8 1.5 %copy.19 = bf16[16,16,16,256]{3,1,2,0:T(8,128)(2,1)} copy(bf16[16,16,16,256]{3,1,0,2:T(8,128)(2,1)S(1)} %bitcast.55) | data formatting | bytes 4194304 | tf_op jit(solution)/shard_map/reshape | solution.py:46
  77.3 12.0 %all-to-all-start.1 = ((bf16[16,16,16,256]{3,1,2,0:T(8,128)(2,1)}), bf16[16,16,16,256]{3,1,2,0:T(8,128)(2,1)}, u32[]{:S(2)}, u32[]{:S(2)}) async-start(bf16[16,16,16,256]{3,1,2,0:T(8,128)(2,1)} %copy.19), calls=%async_computation.1 | async-start | bytes 4194304 | tf_op jit(solution)/shard_map/all_to_all | solution.py:51
  89.3 3.1 %constant_dynamic-update-slice_fusion.8 = bf16[16,9,256,256]{3,2,1,0:T(8,128)(2,1)} fusion(bf16[16,9,256,256]{3,2,1,0:T(8,128)(2,1)} %constant_dynamic-update-slice_fusion.9, bf16[16,1,256,256]{3,2,1,0:T(8,128)(2,1)} %bitcast.54), kind=kLoop, calls=%fused_computation.25 | loop fusion | bytes 4194304
  92.4 0.0 collective-permute-done.1
  92.4 0.6 fusion.12
  93.1 1.5 %constant_dynamic-update-slice_fusion.7 = bf16[16,9,256,256]{3,2,1,0:T(8,128)(2,1)} fusion(bf16[16,9,256,256]{3,2,1,0:T(8,128)(2,1)} %constant_dynamic-update-slice_fusion.8, bf16[16,1,256,256]{3,2,1,0:T(8,128)(2,1)S(1)} %bitcast.62), kind=kLoop, calls=%fused_computation.24 | loop fusion | bytes 4194304
  94.6 1.5 %constant_dynamic-update-slice_fusion.6 = bf16[16,9,256,256]{3,2,1,0:T(8,128)(2,1)} fusion(bf16[16,9,256,256]{3,2,1,0:T(8,128)(2,1)} %constant_dynamic-update-slice_fusion.7, bf16[16,1,256,256]{3,2,1,0:T(8,128)(2,1)S(1)} %bitcast.60), kind=kLoop, calls=%fused_computation.23 | loop fusion | bytes 4194304
  96.1 1.5 %constant_dynamic-update-slice_fusion.5 = bf16[16,9,256,256]{3,2,1,0:T(8,128)(2,1)} fusion(bf16[16,9,256,256]{3,2,1,0:T(8,128)(2,1)} %constant_dynamic-update-slice_fusion.6, bf16[16,1,256,256]{3,2,1,0:T(8,128)(2,1)S(1)} %bitcast.58), kind=kLoop, calls=%fused_computation.22 | loop fusion | bytes 4194304
  97.7 1.5 %constant_dynamic-update-slice_fusion.4 = bf16[16,9,256,256]{3,2,1,0:T(8,128)(2,1)} fusion(bf16[16,9,256,256]{3,2,1,0:T(8,128)(2,1)} %constant_dynamic-update-slice_fusion.5, bf16[16,1,256,256]{3,2,1,0:T(8,128)(2,1)S(1)} %bitcast.56), kind=kLoop, calls=%fused_computation.21 | loop fusion | bytes 4194304 | tf_op jit(solution)/shard_map/stack | solution.py:63
  99.2 19.3 %all-to-all-done.1 = bf16[16,16,16,256]{3,1,2,0:T(8,128)(2,1)} async-done(((bf16[16,16,16,256]{3,1,2,0:T(8,128)(2,1)}), bf16[16,16,16,256]{3,1,2,0:T(8,128)(2,1)}, u32[]{:S(2)}, u32[]{:S(2)}) %all-to-all-start.1) | async-done | bytes 2097184 | tf_op jit(solution)/shard_map/all_to_all | solution.py:51
  118.5 1.9 %convert_reduce_fusion = f32[16,16,256]{2,0,1:T(8,128)S(1)} fusion(bf16[16,16,16,256]{3,1,2,0:T(8,128)(2,1)} %all-to-all-done.1), kind=kLoop, calls=%fused_computation.3 | loop fusion | flops 2031616 | bytes 2359296 | tf_op jit(solution)/shard_map/reduce_sum | solution.py:52
  120.4 3.9 %fusion.4 = f32[16,256,256]{2,1,0:T(8,128)} fusion(f32[16,16,256]{2,0,1:T(8,128)S(1)} %convert_reduce_fusion, bf16[2,16,8,256]{3,2,1,0:T(8,128)(2,1)S(1)} %bitcast.64), kind=kOutput, calls=%fused_computation.9 | convolution fusion | flops 201326592 | bytes 4587520 | tf_op jit(solution)/shard_map/kpr,krn->kpn/dot_general | solution.py:102
  124.3 0.0 copy-start.1
  124.3 16.7 %fusion = bf16[16,256,256]{2,1,0:T(8,128)(2,1)} fusion(f32[16,256,256]{2,1,0:T(8,128)} %fusion.4, bf16[16,9,256,256]{3,2,1,0:T(8,128)(2,1)} %param.11, bf16[16,9,256,256]{3,2,1,0:T(8,128)(2,1)} %constant_dynamic-update-slice_fusion.4), kind=kOutput, calls=%fused_computation.2 | convolution fusion | flops 4833935360 | bytes 44040192 | tf_op jit(solution)/shard_map/kopq,koqn->kpn/dot_general | solution.py:66
  141.0 0.0 copy-done.1
  (6 shorter events, 0.1 us)
Async XLA Ops:
  0.0 25.4 %copy-start = (bf16[65536,16]{0,1:T(8,128)(2,1)S(1)}, bf16[65536,16]{0,1:T(8,128)(2,1)}, u32[]{:S(2)}) copy-start(bf16[65536,16]{0,1:T(8,128)(2,1)} %param.9) | copy-start | bytes 6291460
  2.5 22.9 %collective-permute-start = (bf16[1024,256]{1,0:T(8,128)(2,1)}, bf16[1024,256]{1,0:T(8,128)(2,1)S(1)}, u32[]{:S(2)}, u32[]{:S(2)}) collective-permute-start(bf16[1024,256]{1,0:T(8,128)(2,1)} %get-tuple-element.14), channel_id=1, source_target_pairs={{0,1},{1,2},{2,3},{3,4},{4,5},{5,6},{6,7},{7,8},{8,9},{9,10},{10,1... | collective-permute-start | bytes 1572872 | tf_op jit(solution)/shard_map/ppermute | solution.py:15
  4.4 88.0 %collective-permute-start.1 = (bf16[1024,256]{1,0:T(8,128)(2,1)}, bf16[1024,256]{1,0:T(8,128)(2,1)S(1)}, u32[]{:S(2)}, u32[]{:S(2)}) collective-permute-start(bf16[1024,256]{1,0:T(8,128)(2,1)} %get-tuple-element.13), channel_id=1, source_target_pairs={{1,0},{2,1},{3,2},{4,3},{5,4},{6,5},{7,6},{8,7},{9,8},{10,9},{11,1... | collective-permute-start | bytes 1572872 | tf_op jit(solution)/shard_map/ppermute | solution.py:16
  12.5 9.4 %copy-start.4 = (s32[1,1,512]{2,1,0:T(1,128)S(1)}, s32[1,1,512]{2,1,0:T(1,128)}, u32[]{:S(2)}) copy-start(s32[1,1,512]{2,1,0:T(1,128)} %param.14) | copy-start | bytes 6148
  12.6 9.4 %copy-start.2 = (bf16[1,1,512,16,16]{2,4,3,1,0:T(8,128)(2,1)S(1)}, bf16[1,1,512,16,16]{2,4,3,1,0:T(8,128)(2,1)}, u32[]{:S(2)}) copy-start(bf16[1,1,512,16,16]{2,4,3,1,0:T(8,128)(2,1)} %param.12) | copy-start | bytes 786436
  15.7 18.3 %all-to-all-start = ((bf16[8,16,16,256]{3,2,1,0:T(8,128)(2,1)}), bf16[8,16,16,256]{3,2,1,0:T(8,128)(2,1)}, u32[]{:S(2)}, u32[]{:S(2)}) async-start(bf16[8,16,16,256]{3,2,1,0:T(8,128)(2,1)} %broadcast_in_dim.2), calls=%async_computation | async-start | bytes 2097152 | tf_op jit(solution)/shard_map/all_to_all | solution.py:35
  53.8 9.1 %copy-start.3 = (s32[1,1,512]{2,1,0:T(1,128)S(1)}, s32[1,1,512]{2,1,0:T(1,128)}, u32[]{:S(2)}) copy-start(s32[1,1,512]{2,1,0:T(1,128)} %param.13) | copy-start | bytes 6148
  77.3 41.2 %all-to-all-start.1 = ((bf16[16,16,16,256]{3,1,2,0:T(8,128)(2,1)}), bf16[16,16,16,256]{3,1,2,0:T(8,128)(2,1)}, u32[]{:S(2)}, u32[]{:S(2)}) async-start(bf16[16,16,16,256]{3,1,2,0:T(8,128)(2,1)} %copy.19), calls=%async_computation.1 | async-start | bytes 4194304 | tf_op jit(solution)/shard_map/all_to_all | solution.py:51
  124.3 16.7 %copy-start.1 = (bf16[65536,16]{0,1:T(8,128)(2,1)S(1)}, bf16[65536,16]{0,1:T(8,128)(2,1)}, u32[]{:S(2)}) copy-start(bf16[65536,16]{0,1:T(8,128)(2,1)} %param.9) | copy-start | bytes 6291460
where the time goes:
time: 142 us; the launch traced here: 141 us
  local copies, waits for them, and re-layouts  51.1 us (36%)
  matrix products  39.6 us (28%)
  starting transfers between devices  28.2 us (20%)
  waiting for transfers between devices  19.3 us (14%)
  other arithmetic  1.92 us (1%)
    unnamed x21, local copies, waits for them, and re-layouts  27.3 us
    all_to_all x1, waiting for transfers between devices, sent_and_summed(): lax.all_to_all(parts, axis, split_axis=0, concat_axis=0, tiled=True)  19.3 us
    dot_general x1, matrix products, near_part(): jnp.einsum('kopq,koqn->kpn', near_blocks, stacked, preferred_element_type...  16.7 us
    dot_general x1, matrix products, far_part(): jnp.dot(one_hot, block_terms.reshape(slots, rank_size * panel_cols), prec...  12.9 us
    all_to_all x1, starting transfers between devices, sent_and_summed(): lax.all_to_all(parts, axis, split_axis=0, concat_axis=0, tiled=True)  12 us
    dot_general x1, local copies, waits for them, and re-layouts, far_part(): jnp.dot(one_hot, block_terms.reshape(slots, rank_size * panel_cols), prec...  9.05 us
    ppermute x1, starting transfers between devices, padded_2(): lax.ppermute(leading, axis, [(b, a) for a, b in up])  8.15 us
    all_to_all x1, starting transfers between devices, copy_for_each(): lax.all_to_all(jnp.broadcast_to(array[None], (peers, *array.shape)), axis...  6.16 us
  transfers between devices with their start and end apart: 4, of which 1 were waited for; matrix products, arithmetic and copies ran while one was open for 48% of the time, Pallas kernels for 0%

commit v1 on v0

v1 whole, which is shorter than its diff:
```python
import functools

import jax
import jax.numpy as jnp
from jax import lax
from jax.experimental import pallas as pl
from jax.experimental.pallas import tpu as pltpu
from jax.sharding import Mesh, PartitionSpec as P

F32, BF16, I32 = jnp.float32, jnp.bfloat16, jnp.int32
ROW, COL = ("zl", "y"), ("x", "zh", "core")
NT = (((1,), (1,)), ((), ()))
TN = (((0,), (0,)), ((), ()))
VMEM = pl.BlockSpec(memory_space=pltpu.VMEM)
SMEM = pl.BlockSpec(memory_space=pltpu.SMEM)


def cost(flops, nbytes):
    return pl.CostEstimate(flops=flops, bytes_accessed=nbytes, transcendentals=0)


def params(mib):
    return pltpu.CompilerParams(vmem_limit_bytes=mib << 20)


def coeff_kernel(peers, leaf, rank, half, panel_ref, vt_ref, send_ref, head_ref, tail_ref):
    rows = panel_ref.shape[0]
    for k in range(rows // leaf):
        span = pl.ds(k * leaf, leaf)
        value = jnp.dot(vt_ref[:, span], panel_ref[span, :], preferred_element_type=F32).astype(BF16)
        for peer in range(peers):
            send_ref[peer, pl.ds(k * rank, rank), :] = value
    head_ref[...] = panel_ref[pl.ds(0, half * leaf), :]
    tail_ref[...] = panel_ref[pl.ds(rows - half * leaf, half * leaf), :]


def prep_kernel(per_dev, rank, groups, info_ref, rows_ref, cols_ref, x_ref, ct_ref, table_ref):
    slots = rows_ref.shape[1]
    count, core = info_ref[0], info_ref[1]
    lane = lax.broadcasted_iota(I32, (1, slots), 1)
    live = lane < count
    rows = rows_ref[...]
    dest, local = rows // per_dev, rows % per_dev
    other = jnp.where(dest % 2 == core, 0, 1)
    row_key = other * (groups // 2) + (dest // 2) * per_dev + local
    key = jnp.where(live, row_key, groups) * slots + lane
    down = lax.broadcasted_iota(I32, (slots, slots), 0)
    across = lax.broadcasted_iota(I32, (slots, slots), 1)
    key_down = jnp.sum(jnp.where(down == across, key, 0), axis=1, keepdims=True)
    place = jnp.sum((key_down < key).astype(I32), axis=0, keepdims=True)
    place = jnp.where(live, place, -1)
    pick = (down == place).astype(F32).astype(BF16)
    value = lax.dot_general(pick, x_ref[...], NT, preferred_element_type=F32)
    width = value.shape[1]
    k_of = lax.broadcasted_iota(I32, value.shape, 0)
    i_of = lax.broadcasted_iota(I32, value.shape, 1) // rank
    step = 1
    while step < rank:
        k_bit, i_bit = (k_of // step) % 2, (i_of // step) % 2
        ahead = pltpu.roll(pltpu.roll(value, slots - step, 0), step * rank, 1)
        behind = pltpu.roll(pltpu.roll(value, step, 0), width - step * rank, 1)
        value = jnp.where(k_bit == i_bit, value, jnp.where(k_bit == 0, ahead, behind))
        step *= 2
    ct_ref[...] = value.astype(BF16)
    top = jnp.max(jnp.where(live, row_key, 0))
    pair = jnp.concatenate([cols_ref[...], row_key] + [jnp.zeros_like(row_key)] * 6, axis=0)
    table = lax.dot_general(pair.astype(F32).astype(BF16), pick, NT, preferred_element_type=F32).astype(I32)
    which = lax.broadcasted_iota(I32, table.shape, 0)
    past = lax.broadcasted_iota(I32, table.shape, 1) >= count
    table_ref[...] = jnp.where(past & (which == 1), top, table)


def block_kernel(rank, tile, unroll, table_ref, ct_ref, g_ref, own_ref, other_ref, out_ref):
    slots = table_ref.shape[1]
    cols = g_ref.shape[1]
    out_ref[...] = jnp.zeros_like(out_ref)
    width = tile * rank
    group = lax.broadcasted_iota(I32, (rank, width), 1) // rank
    masks = [(group == k).astype(F32).astype(BF16) for k in range(tile)]
    halves = ct_ref.shape[1] // width

    def body(step, carry):
        acc, last = carry
        for u in range(unroll):
            for h in range(halves):
                base = (step * unroll + u) * tile * halves + h * tile
                ct = ct_ref[pl.ds(pl.multiple_of((step * unroll + u) * rank, rank), rank), h * width : (h + 1) * width]
                lhs = jnp.concatenate([ct * m for m in masks], axis=0)
                rhs = jnp.concatenate(
                    [
                        g_ref[pl.ds(pl.multiple_of(table_ref[0, base + k] * rank, rank), rank), :]
                        for k in range(tile)
                    ],
                    axis=0,
                )
                terms = jnp.dot(lhs, rhs, preferred_element_type=F32)
                for k in range(tile):
                    row = table_ref[1, base + k]
                    term = terms[k * rank : (k + 1) * rank, :]
                    acc = term + jnp.where(row == last, acc, 0.0)
                    last = row
                    out_ref[pl.ds(pl.multiple_of(row * rank, rank), rank), :] = acc.astype(BF16)
        return acc, last

    steps = slots // (tile * halves * unroll)
    lax.fori_loop(0, steps, body, (jnp.zeros((rank, cols), F32), jnp.int32(-1)))
    size = own_ref.shape[0]
    own_ref[...] = out_ref[pl.ds(0, size), :]
    other_ref[...] = out_ref[pl.ds(size, size), :]


def pair_kernel(a_ref, b_ref, out_ref):
    out_ref[...] = (a_ref[...].astype(F32) + b_ref[...].astype(F32)).astype(BF16)


def near_kernel(half, leaf, nb_ref, panel_ref, low_ref, high_ref, out_ref, window):
    k = pl.program_id(0)
    rows, edge = panel_ref.shape[0], half * leaf

    @pl.when(k == 0)
    def _():
        window[pl.ds(0, edge), :] = low_ref[...]
        window[pl.ds(edge, rows), :] = panel_ref[...]
        window[pl.ds(edge + rows, edge), :] = high_ref[...]

    total = None
    for o in range(nb_ref.shape[1]):
        rhs = window[pl.ds(pl.multiple_of((k + o) * leaf, leaf), leaf), :]
        term = jnp.dot(nb_ref[0, o], rhs, preferred_element_type=F32)
        total = term if total is None else total + term
    out_ref[...] = total


def final_kernel(place_ref, parts_ref, ut_ref, near_ref, out_ref):
    coupled = parts_ref[0].astype(F32)
    for p in range(1, parts_ref.shape[0]):
        coupled = coupled + parts_ref[p].astype(F32)
    high = coupled.astype(BF16)
    low = (coupled - high.astype(F32)).astype(BF16)
    ut = ut_ref[...]
    far = lax.dot_general(
        jnp.concatenate([ut, ut], axis=0), jnp.concatenate([high, low], axis=0), TN, preferred_element_type=F32
    )
    out_ref[...] = (near_ref[...] + far).astype(BF16)


def on_device(panel, row_basis, col_basis, near_blocks, couplings, blk_rows, blk_cols, blk_count):
    rows, cols = panel.shape
    clusters, near_count, leaf, _ = near_blocks.shape
    rank, slots = col_basis.shape[1], couplings.shape[2]
    half = near_count // 2
    row_peers, col_peers = lax.axis_size(ROW), lax.axis_size(COL)
    groups = col_peers * clusters
    core = lax.axis_index("core")

    send, head, tail = pl.pallas_call(
        functools.partial(coeff_kernel, row_peers, leaf, rank, half),
        out_shape=(
            jax.ShapeDtypeStruct((row_peers, clusters * rank, cols), BF16),
            jax.ShapeDtypeStruct((half * leaf, cols), BF16),
            jax.ShapeDtypeStruct((half * leaf, cols), BF16),
        ),
        in_specs=[VMEM, VMEM],
        out_specs=(VMEM, VMEM, VMEM),
        compiler_params=params(16),
        cost_estimate=cost(2 * rows * rank * cols, 5 << 20),
        name="coeffs",
    )(panel, col_basis.T)
    gathered = lax.all_to_all(send, ROW, 0, 0, tiled=True)

    every = ROW + COL
    peers = lax.axis_size(every)
    up = [(i, i + 1) for i in range(peers - 1)]
    low = lax.ppermute(tail, every, up)
    high = lax.ppermute(head, every, [(b, a) for a, b in up])

    info = jnp.stack([blk_count.reshape(()), core.astype(I32)])
    x = jnp.transpose(couplings.reshape(slots, rank, rank), (1, 2, 0)).reshape(rank * rank, slots)
    ct, table = pl.pallas_call(
        functools.partial(prep_kernel, clusters, rank, groups),
        out_shape=(jax.ShapeDtypeStruct((slots, rank * rank), BF16), jax.ShapeDtypeStruct((8, slots), I32)),
        in_specs=[SMEM, VMEM, VMEM, VMEM],
        out_specs=(VMEM, VMEM),
        compiler_params=params(24),
        cost_estimate=cost(2 * slots * slots * rank * rank, 1 << 20),
        name="prep",
    )(info, blk_rows.reshape(1, slots), blk_cols.reshape(1, slots), x)

    mine, theirs = pl.pallas_call(
        functools.partial(block_kernel, rank, 128 // rank, 4),
        out_shape=[jax.ShapeDtypeStruct((groups // 2 * rank, cols), BF16)] * 2,
        in_specs=[SMEM, VMEM, VMEM],
        out_specs=[VMEM, VMEM],
        scratch_shapes=[pltpu.VMEM((groups * rank, cols), BF16)],
        compiler_params=params(24),
        cost_estimate=cost(2 * slots * rank * 128 * cols, 4 << 20),
        name="blocks",
    )(table, ct, gathered.reshape(row_peers * clusters * rank, cols))

    swapped = lax.ppermute(theirs, "core", [(0, 1), (1, 0)])
    summed = pl.pallas_call(
        pair_kernel,
        out_shape=jax.ShapeDtypeStruct(mine.shape, BF16),
        in_specs=[VMEM, VMEM],
        out_specs=VMEM,
        compiler_params=params(16),
        cost_estimate=cost(mine.size, 3 << 20),
        name="pair",
    )(mine, swapped)
    parts = lax.all_to_all(
        summed.reshape(col_peers // 2, clusters * rank, cols), ("x", "zh"), 0, 0, tiled=True
    )

    near = pl.pallas_call(
        functools.partial(near_kernel, half, leaf),
        out_shape=jax.ShapeDtypeStruct((rows, cols), F32),
        grid=(clusters,),
        in_specs=[
            pl.BlockSpec((1, near_count, leaf, leaf), lambda k: (k, 0, 0, 0)),
            pl.BlockSpec((rows, cols), lambda k: (0, 0)),
            pl.BlockSpec((half * leaf, cols), lambda k: (0, 0)),
            pl.BlockSpec((half * leaf, cols), lambda k: (0, 0)),
        ],
        out_specs=pl.BlockSpec((leaf, cols), lambda k: (k, 0)),
        scratch_shapes=[pltpu.VMEM((rows + 2 * half * leaf, cols), BF16)],
        compiler_params=params(32),
        cost_estimate=cost(2 * clusters * near_count * leaf * leaf * cols, 28 << 20),
        name="near",
    )(near_blocks, panel, low, high)

    place = lax.axis_index(COL).astype(I32).reshape(1)
    return pl.pallas_call(
        final_kernel,
        out_shape=jax.ShapeDtypeStruct((rows, cols), BF16),
        grid_spec=pltpu.PrefetchScalarGridSpec(
            num_scalar_prefetch=1,
            grid=(clusters,),
            in_specs=[
                pl.BlockSpec((col_peers // 2, rank, cols), lambda k, at: (0, k, 0)),
                pl.BlockSpec((rank, leaf), lambda k, at: (0, at[0] * clusters + k)),
                pl.BlockSpec((leaf, cols), lambda k, at: (k, 0)),
            ],
            out_specs=pl.BlockSpec((leaf, cols), lambda k, at: (k, 0)),
        ),
        compiler_params=params(16),
        cost_estimate=cost(4 * rows * rank * cols, 8 << 20),
        name="final",
    )(place, parts, row_basis.T, near)


def solution(mesh):
    devices = mesh.devices.reshape(2, 4, 4, 2, 2)
    fine = Mesh(devices, ("zl", "y", "x", "zh", "core"))
    placed = (
        P((*ROW, *COL), None),
        P(ROW, None),
        P((*ROW, *COL), None),
        P((*ROW, *COL), None, None, None),
        P(ROW, COL, None, None, None),
        P(ROW, COL, None),
        P(ROW, COL, None),
        P(ROW, COL),
    )
    return jax.shard_map(
        on_device, mesh=fine, in_specs=placed, out_specs=P((*ROW, *COL), None), check_vma=False
    )
```

time: 142 us -> 89.4 us (0.63)
  the two profiles are of different devices: /device:TPU:16 before, /device:TPU:9 now
where the time goes in v1:
time: 89.4 us; the launch traced here: 88.8 us
  Pallas kernels  30.8 us (34%)
  waiting for transfers between devices  28.7 us (32%)
  starting transfers between devices  19.3 us (22%)
  local copies, waits for them, and re-layouts  9.2 us (10%)
    pallas_call x1, Pallas kernels, on_device(): pl.pallas_call(functools.partial(near_kernel, half, leaf), out_shape=jax....  15.7 us
    ppermute x1, waiting for transfers between devices, on_device(): low = lax.ppermute(tail, every, up)  14.4 us
    all_to_all x1, waiting for transfers between devices, on_device(): gathered = lax.all_to_all(send, ROW, 0, 0, tiled=True)  11 us
    unnamed x20, local copies, waits for them, and re-layouts  9.2 us
    pallas_call x1, Pallas kernels, on_device(): pl.pallas_call(final_kernel, out_shape=jax.ShapeDtypeStruct((rows, cols),...  7.22 us
    all_to_all x1, starting transfers between devices, on_device(): gathered = lax.all_to_all(send, ROW, 0, 0, tiled=True)  5.71 us
    ppermute x1, starting transfers between devices, on_device(): low = lax.ppermute(tail, every, up)  5.11 us
    all_to_all x1, starting transfers between devices, on_device(): lax.all_to_all(summed.reshape(col_peers // 2, clusters * rank, cols), ('x...  4.33 us
  transfers between devices with their start and end apart: 5, of which 3 were waited for; matrix products, arithmetic and copies ran while one was open for 0% of the time, Pallas kernels for 20%

profile of v1, /device:TPU:9, one launch (start us, length us, event | category | flops | bytes accessed | tf_op | source)
XLA Modules:
  0.0 88.8 jit_solution(14247613804987223876)
XLA Ops:
  0.0 0.0 copy-start.2
  0.0 1.6 %copy-done.2 = bf16[4096,256]{1,0:T(8,128)(2,1)S(1)} copy-done((bf16[4096,256]{1,0:T(8,128)(2,1)S(1)}, bf16[4096,256]{1,0:T(8,128)(2,1)}, u32[]{:S(2)}) %copy-start.2) | copy-done | bytes 2097176
  1.6 0.0 copy-start.6
  1.6 0.9 %copy-done.6 = bf16[4096,16]{0,1:T(8,128)(2,1)S(1)} copy-done((bf16[4096,16]{0,1:T(8,128)(2,1)S(1)}, bf16[4096,16]{0,1:T(8,128)(2,1)}, u32[]{:S(2)}) %copy-start.6) | copy-done | bytes 131096
  2.5 0.0 copy-start.7
  2.5 0.0 copy-start.8
  2.5 0.0 copy-start.9
  2.5 1.7 %coeffs.1 = (bf16[8,256,256]{2,1,0:T(8,128)(2,1)}, bf16[1024,256]{1,0:T(8,128)(2,1)}, bf16[1024,256]{1,0:T(8,128)(2,1)}) custom-call(bf16[4096,256]{1,0:T(8,128)(2,1)S(1)} %copy-done.2, bf16[16,4096]{1,0:T(8,128)(2,1)S(1)} %bitcast.18), custom_call_target="tpu_custom_call" | custom-call | flops 33554432 | bytes 5242880 | tf_op jit(solution)/shard_map/coeffs/pallas_call | solution.py:156
  4.2 5.7 %all-to-all-start = ((bf16[8,256,256]{2,1,0:T(8,128)(2,1)}), bf16[8,256,256]{2,1,0:T(8,128)(2,1)S(1)}, u32[]{:S(2)}, u32[]{:S(2)}) async-start(bf16[8,256,256]{2,1,0:T(8,128)(2,1)} %get-tuple-element.14), calls=%async_computation | async-start | bytes 2097152 | tf_op jit(solution)/shard_map/all_to_all | solution.py:169
  10.5 0.1 pad_add_fusion.info_ref
  10.6 0.0 copy-done.7
  10.6 0.0 copy-done.8
  10.6 0.0 copy-done.9
  10.6 1.9 %prep.1 = (bf16[512,256]{1,0:T(8,128)(2,1)S(1)}, s32[8,512]{1,0:T(8,128)S(1)}) custom-call(s32[2]{0:T(128)S(1)} %pad_add_fusion.info_ref, s32[1,512]{1,0:T(1,128)S(1)} %bitcast.20, s32[1,512]{1,0:T(1,128)S(1)} %bitcast.21, bf16[256,512]{1,0:T(8,128)(2,1)S(1)} %bitcast.19), custom_call_target="tpu_custom_call" | custom-call | flops 134217728 | bytes 1048576 | tf_op jit(solution)/shard_map/prep/pallas_call | solution.py:179
  12.5 11.0 %all-to-all-done = bf16[8,256,256]{2,1,0:T(8,128)(2,1)S(1)} async-done(((bf16[8,256,256]{2,1,0:T(8,128)(2,1)}), bf16[8,256,256]{2,1,0:T(8,128)(2,1)S(1)}, u32[]{:S(2)}, u32[]{:S(2)}) %all-to-all-start) | async-done | bytes 1048608 | tf_op jit(solution)/shard_map/all_to_all | solution.py:169
  23.5 4.1 %blocks.1 = (bf16[2048,256]{1,0:T(8,128)(2,1)S(1)}, bf16[2048,256]{1,0:T(8,128)(2,1)S(1)}) custom-call(s32[8,512]{1,0:T(8,128)S(1)} %get-tuple-element.12.table_ref, bf16[512,256]{1,0:T(8,128)(2,1)S(1)} %get-tuple-element.13.ct_ref, bf16[2048,256]{1,0:T(8,128)(2,1)S(1)} %bitcast.17), custom_call_target="tpu_custom_call" | custom-call | flops 536870912 | bytes 4194304 | tf_op jit(solution)/shard_map/blocks/pallas_call | solution.py:189
  27.6 2.2 %collective-permute-start = (bf16[2048,256]{1,0:T(8,128)(2,1)S(1)}, bf16[2048,256]{1,0:T(8,128)(2,1)S(1)}, u32[]{:S(2)}, u32[]{:S(2)}) collective-permute-start(bf16[2048,256]{1,0:T(8,128)(2,1)S(1)} %get-tuple-element.16), channel_id=1, source_target_pairs={{0,1},{1,0},{2,3},{3,2},{4,5},{5,4},{6,7},{7,6},{8,9},{9,8},{10,11... | collective-permute-start | bytes 3145736 | tf_op jit(solution)/shard_map/ppermute | solution.py:200
  29.8 5.1 %collective-permute-start.1 = (bf16[1024,256]{1,0:T(8,128)(2,1)}, bf16[1024,256]{1,0:T(8,128)(2,1)}, u32[]{:S(2)}, u32[]{:S(2)}) collective-permute-start(bf16[1024,256]{1,0:T(8,128)(2,1)} %get-tuple-element.17), channel_id=1, source_target_pairs={{0,1},{1,2},{2,3},{3,4},{4,5},{5,6},{6,7},{7,8},{8,9},{9,10},{10,1... | collective-permute-start | bytes 1572872 | tf_op jit(solution)/shard_map/ppermute | solution.py:174
  34.9 1.9 %collective-permute-start.2 = (bf16[1024,256]{1,0:T(8,128)(2,1)}, bf16[1024,256]{1,0:T(8,128)(2,1)}, u32[]{:S(2)}, u32[]{:S(2)}) collective-permute-start(bf16[1024,256]{1,0:T(8,128)(2,1)} %get-tuple-element.18), channel_id=1, source_target_pairs={{1,0},{2,1},{3,2},{4,3},{5,4},{6,5},{7,6},{8,7},{9,8},{10,9},{11,1... | collective-permute-start | bytes 1572872 | tf_op jit(solution)/shard_map/ppermute | solution.py:175
  36.8 0.0 collective-permute-done.b_ref
  36.8 0.0 copy-start.3
  36.9 0.2 pair.1
  37.1 0.0 copy-start.4
  37.1 1.0 %copy-done.4 = bf16[2048,256]{1,0:T(8,128)(2,1)} copy-done((bf16[2048,256]{1,0:T(8,128)(2,1)}, bf16[2048,256]{1,0:T(8,128)(2,1)S(1)}, u32[]{:S(2)}) %copy-start.4) | copy-done | bytes 1048600
  38.1 4.3 %all-to-all-start.1 = ((bf16[8,256,256]{2,1,0:T(8,128)(2,1)}), bf16[8,256,256]{2,1,0:T(8,128)(2,1)S(1)}, u32[]{:S(2)}, u32[]{:S(2)}) async-start(bf16[8,256,256]{2,1,0:T(8,128)(2,1)} %bitcast.15), calls=%async_computation.1 | async-start | bytes 2097152 | tf_op jit(solution)/shard_map/all_to_all | solution.py:210
  42.4 14.4 %collective-permute-done.1.low_ref = bf16[1024,256]{1,0:T(8,128)(2,1)} collective-permute-done((bf16[1024,256]{1,0:T(8,128)(2,1)}, bf16[1024,256]{1,0:T(8,128)(2,1)}, u32[]{:S(2)}, u32[]{:S(2)}) %collective-permute-start.1) | collective-permute-done | bytes 524320 | tf_op jit(solution)/shard_map/ppermute | solution.py:174
  56.8 3.4 %collective-permute-done.2.high_ref = bf16[1024,256]{1,0:T(8,128)(2,1)} collective-permute-done((bf16[1024,256]{1,0:T(8,128)(2,1)}, bf16[1024,256]{1,0:T(8,128)(2,1)}, u32[]{:S(2)}, u32[]{:S(2)}) %collective-permute-start.2) | collective-permute-done | bytes 524320 | tf_op jit(solution)/shard_map/ppermute | solution.py:175
  60.1 0.0 copy-done.3
  60.1 15.7 %near.1.near_ref = f32[4096,256]{1,0:T(8,128)S(1)} custom-call(bf16[16,9,256,256]{3,2,1,0:T(8,128)(2,1)} %nb_ref.1, bf16[4096,256]{1,0:T(8,128)(2,1)S(1)} %copy-done.3, bf16[1024,256]{1,0:T(8,128)(2,1)} %collective-permute-done.1.low_ref, bf16[1024,256]{1,0:T(8,128)(2,1)} %collective-permute-done.2.high_ref), custom_call_target="tpu_custom_call" | custom-call | flops 4831838208 | bytes 29360128 | tf_op jit(solution)/shard_map/near/pallas_call | solution.py:214
  75.8 0.0 copy-start
  75.8 1.9 %copy-done = f32[4096,256]{1,0:T(8,128)} copy-done((f32[4096,256]{1,0:T(8,128)}, f32[4096,256]{1,0:T(8,128)S(1)}, u32[]{:S(2)}) %copy-start) | copy-done | bytes 4194328
  77.8 0.0 all-to-all-done.1.parts_ref
  77.8 0.0 copy-start.1
  77.8 2.2 %copy-done.1 = f32[4096,256]{1,0:T(8,128)S(1)} copy-done((f32[4096,256]{1,0:T(8,128)S(1)}, f32[4096,256]{1,0:T(8,128)}, u32[]{:S(2)}) %copy-start.1) | copy-done | bytes 4194328
  80.0 0.0 copy-start.5
  80.0 1.6 %copy-done.5 = bf16[65536,16]{0,1:T(8,128)(2,1)S(1)} copy-done((bf16[65536,16]{0,1:T(8,128)(2,1)S(1)}, bf16[65536,16]{0,1:T(8,128)(2,1)}, u32[]{:S(2)}) %copy-start.5) | copy-done | bytes 2097176
  81.6 7.2 %final.1 = bf16[4096,256]{1,0:T(8,128)(2,1)} custom-call(s32[1]{0:T(128)} %bitcast.place_ref, bf16[8,256,256]{2,1,0:T(8,128)(2,1)S(1)} %all-to-all-done.1.parts_ref, bf16[16,65536]{1,0:T(8,128)(2,1)S(1)} %bitcast.16, f32[4096,256]{1,0:T(8,128)S(1)} %copy-done.1), custom_call_target="tpu_custom_call" | custom-call | flops 67108864 | bytes 8388608 | tf_op jit(solution)/shard_map/final/pallas_call | solution.py:232
Async XLA Ops:
  0.0 1.6 %copy-start.2 = (bf16[4096,256]{1,0:T(8,128)(2,1)S(1)}, bf16[4096,256]{1,0:T(8,128)(2,1)}, u32[]{:S(2)}) copy-start(bf16[4096,256]{1,0:T(8,128)(2,1)} %panel_ref.3) | copy-start | bytes 6291460
  1.6 0.9 %copy-start.6 = (bf16[4096,16]{0,1:T(8,128)(2,1)S(1)}, bf16[4096,16]{0,1:T(8,128)(2,1)}, u32[]{:S(2)}) copy-start(bf16[4096,16]{0,1:T(8,128)(2,1)} %param.10) | copy-start | bytes 393220
  2.5 8.1 %copy-start.7 = (bf16[1,1,512,16,16]{2,4,3,1,0:T(8,128)(2,1)S(1)}, bf16[1,1,512,16,16]{2,4,3,1,0:T(8,128)(2,1)}, u32[]{:S(2)}) copy-start(bf16[1,1,512,16,16]{2,4,3,1,0:T(8,128)(2,1)} %param.12) | copy-start | bytes 786436
  2.5 8.1 %copy-start.8 = (s32[1,1,512]{2,1,0:T(1,128)S(1)}, s32[1,1,512]{2,1,0:T(1,128)}, u32[]{:S(2)}) copy-start(s32[1,1,512]{2,1,0:T(1,128)} %param.13) | copy-start | bytes 6148
  2.5 8.1 %copy-start.9 = (s32[1,1,512]{2,1,0:T(1,128)S(1)}, s32[1,1,512]{2,1,0:T(1,128)}, u32[]{:S(2)}) copy-start(s32[1,1,512]{2,1,0:T(1,128)} %param.14) | copy-start | bytes 6148
  4.2 19.4 %all-to-all-start = ((bf16[8,256,256]{2,1,0:T(8,128)(2,1)}), bf16[8,256,256]{2,1,0:T(8,128)(2,1)S(1)}, u32[]{:S(2)}, u32[]{:S(2)}) async-start(bf16[8,256,256]{2,1,0:T(8,128)(2,1)} %get-tuple-element.14), calls=%async_computation | async-start | bytes 2097152 | tf_op jit(solution)/shard_map/all_to_all | solution.py:169
  27.6 9.2 %collective-permute-start = (bf16[2048,256]{1,0:T(8,128)(2,1)S(1)}, bf16[2048,256]{1,0:T(8,128)(2,1)S(1)}, u32[]{:S(2)}, u32[]{:S(2)}) collective-permute-start(bf16[2048,256]{1,0:T(8,128)(2,1)S(1)} %get-tuple-element.16), channel_id=1, source_target_pairs={{0,1},{1,0},{2,3},{3,2},{4,5},{5,4},{6,7},{7,6},{8,9},{9,8},{10,11... | collective-permute-start | bytes 3145736 | tf_op jit(solution)/shard_map/ppermute | solution.py:200
  29.8 27.0 %collective-permute-start.1 = (bf16[1024,256]{1,0:T(8,128)(2,1)}, bf16[1024,256]{1,0:T(8,128)(2,1)}, u32[]{:S(2)}, u32[]{:S(2)}) collective-permute-start(bf16[1024,256]{1,0:T(8,128)(2,1)} %get-tuple-element.17), channel_id=1, source_target_pairs={{0,1},{1,2},{2,3},{3,4},{4,5},{5,6},{6,7},{7,8},{8,9},{9,10},{10,1... | collective-permute-start | bytes 1572872 | tf_op jit(solution)/shard_map/ppermute | solution.py:174
  34.9 25.2 %collective-permute-start.2 = (bf16[1024,256]{1,0:T(8,128)(2,1)}, bf16[1024,256]{1,0:T(8,128)(2,1)}, u32[]{:S(2)}, u32[]{:S(2)}) collective-permute-start(bf16[1024,256]{1,0:T(8,128)(2,1)} %get-tuple-element.18), channel_id=1, source_target_pairs={{1,0},{2,1},{3,2},{4,3},{5,4},{6,5},{7,6},{8,7},{9,8},{10,9},{11,1... | collective-permute-start | bytes 1572872 | tf_op jit(solution)/shard_map/ppermute | solution.py:175
  36.8 23.3 %copy-start.3 = (bf16[4096,256]{1,0:T(8,128)(2,1)S(1)}, bf16[4096,256]{1,0:T(8,128)(2,1)}, u32[]{:S(2)}) copy-start(bf16[4096,256]{1,0:T(8,128)(2,1)} %panel_ref.3) | copy-start | bytes 6291460
  37.1 1.0 %copy-start.4 = (bf16[2048,256]{1,0:T(8,128)(2,1)}, bf16[2048,256]{1,0:T(8,128)(2,1)S(1)}, u32[]{:S(2)}) copy-start(bf16[2048,256]{1,0:T(8,128)(2,1)S(1)} %pair.1) | copy-start | bytes 3145732
  38.1 39.7 %all-to-all-start.1 = ((bf16[8,256,256]{2,1,0:T(8,128)(2,1)}), bf16[8,256,256]{2,1,0:T(8,128)(2,1)S(1)}, u32[]{:S(2)}, u32[]{:S(2)}) async-start(bf16[8,256,256]{2,1,0:T(8,128)(2,1)} %bitcast.15), calls=%async_computation.1 | async-start | bytes 2097152 | tf_op jit(solution)/shard_map/all_to_all | solution.py:210
  75.8 2.0 %copy-start = (f32[4096,256]{1,0:T(8,128)}, f32[4096,256]{1,0:T(8,128)S(1)}, u32[]{:S(2)}) copy-start(f32[4096,256]{1,0:T(8,128)S(1)} %near.1.near_ref) | copy-start | bytes 12582916
  77.8 2.2 %copy-start.1 = (f32[4096,256]{1,0:T(8,128)S(1)}, f32[4096,256]{1,0:T(8,128)}, u32[]{:S(2)}) copy-start(f32[4096,256]{1,0:T(8,128)} %copy-done) | copy-start | bytes 12582916
  80.0 1.6 %copy-start.5 = (bf16[65536,16]{0,1:T(8,128)(2,1)S(1)}, bf16[65536,16]{0,1:T(8,128)(2,1)}, u32[]{:S(2)}) copy-start(bf16[65536,16]{0,1:T(8,128)(2,1)} %param.9) | copy-start | bytes 6291460

commit v2 on v1

--- a/solution.py
+++ b/solution.py
@@ -7,6 +7,7 @@
 from jax.experimental.pallas import tpu as pltpu
 from jax.sharding import Mesh, PartitionSpec as P
 
+
 F32, BF16, I32 = jnp.float32, jnp.bfloat16, jnp.int32
 ROW, COL = ("zl", "y"), ("x", "zh", "core")
 NT = (((1,), (1,)), ((), ()))
@@ -23,15 +24,21 @@
     return pltpu.CompilerParams(vmem_limit_bytes=mib << 20)
 
 
-def coeff_kernel(peers, leaf, rank, half, panel_ref, vt_ref, send_ref, head_ref, tail_ref):
-    rows = panel_ref.shape[0]
-    for k in range(rows // leaf):
+def coeff_kernel(peers, leaf, rank, panel_ref, vt_ref, send_ref, head_ref, tail_ref):
+    step = pl.program_id(0)
+    for k in range(panel_ref.shape[0] // leaf):
         span = pl.ds(k * leaf, leaf)
         value = jnp.dot(vt_ref[:, span], panel_ref[span, :], preferred_element_type=F32).astype(BF16)
         for peer in range(peers):
             send_ref[peer, pl.ds(k * rank, rank), :] = value
-    head_ref[...] = panel_ref[pl.ds(0, half * leaf), :]
-    tail_ref[...] = panel_ref[pl.ds(rows - half * leaf, half * leaf), :]
+
+    @pl.when(step == 0)
+    def _():
+        head_ref[...] = panel_ref[...]
+
+    @pl.when(step == pl.num_programs(0) - 1)
+    def _():
+        tail_ref[...] = panel_ref[...]
 
 
 def prep_kernel(per_dev, rank, groups, info_ref, rows_ref, cols_ref, x_ref, ct_ref, table_ref):
@@ -114,34 +121,35 @@
 
 
 def near_kernel(half, leaf, nb_ref, panel_ref, low_ref, high_ref, out_ref, window):
-    k = pl.program_id(0)
+    step = pl.program_id(0)
     rows, edge = panel_ref.shape[0], half * leaf
-
-    @pl.when(k == 0)
+    held, near_count = nb_ref.shape[:2]
+
+    @pl.when(step == 0)
     def _():
         window[pl.ds(0, edge), :] = low_ref[...]
         window[pl.ds(edge, rows), :] = panel_ref[...]
         window[pl.ds(edge + rows, edge), :] = high_ref[...]
 
-    total = None
-    for o in range(nb_ref.shape[1]):
-        rhs = window[pl.ds(pl.multiple_of((k + o) * leaf, leaf), leaf), :]
-        term = jnp.dot(nb_ref[0, o], rhs, preferred_element_type=F32)
-        total = term if total is None else total + term
-    out_ref[...] = total
-
-
-def final_kernel(place_ref, parts_ref, ut_ref, near_ref, out_ref):
-    coupled = parts_ref[0].astype(F32)
-    for p in range(1, parts_ref.shape[0]):
-        coupled = coupled + parts_ref[p].astype(F32)
-    high = coupled.astype(BF16)
-    low = (coupled - high.astype(F32)).astype(BF16)
-    ut = ut_ref[...]
-    far = lax.dot_general(
-        jnp.concatenate([ut, ut], axis=0), jnp.concatenate([high, low], axis=0), TN, preferred_element_type=F32
-    )
-    out_ref[...] = (near_ref[...] + far).astype(BF16)
+    for c in range(held):
+        lhs = jnp.concatenate([nb_ref[c, o] for o in range(near_count)], axis=1)
+        rhs = window[pl.ds(pl.multiple_of((step * held + c) * leaf, leaf), near_count * leaf), :]
+        out_ref[pl.ds(c * leaf, leaf), :] = jnp.dot(lhs, rhs, preferred_element_type=F32)
+
+
+def final_kernel(rank, leaf, place_ref, parts_ref, ut_ref, near_ref, out_ref):
+    for k in range(near_ref.shape[0] // leaf):
+        span, ranks = pl.ds(k * leaf, leaf), pl.ds(k * rank, rank)
+        coupled = parts_ref[0, ranks, :].astype(F32)
+        for p in range(1, parts_ref.shape[0]):
+            coupled = coupled + parts_ref[p, ranks, :].astype(F32)
+        high = coupled.astype(BF16)
+        low = (coupled - high.astype(F32)).astype(BF16)
+        ut = ut_ref[:, span]
+        far = lax.dot_general(
+            jnp.concatenate([ut, ut], axis=0), jnp.concatenate([high, low], axis=0), TN, preferred_element_type=F32
+        )
+        out_ref[span, :] = (near_ref[span, :] + far).astype(BF16)
 
 
 def on_device(panel, row_basis, col_basis, near_blocks, couplings, blk_rows, blk_cols, blk_count):
@@ -153,16 +161,22 @@
     groups = col_peers * clusters
     core = lax.axis_index("core")
 
+    edge = half * leaf
     send, head, tail = pl.pallas_call(
-        functools.partial(coeff_kernel, row_peers, leaf, rank, half),
+        functools.partial(coeff_kernel, row_peers, leaf, rank),
         out_shape=(
             jax.ShapeDtypeStruct((row_peers, clusters * rank, cols), BF16),
-            jax.ShapeDtypeStruct((half * leaf, cols), BF16),
-            jax.ShapeDtypeStruct((half * leaf, cols), BF16),
+            jax.ShapeDtypeStruct((edge, cols), BF16),
+            jax.ShapeDtypeStruct((edge, cols), BF16),
         ),
-        in_specs=[VMEM, VMEM],
-        out_specs=(VMEM, VMEM, VMEM),
-        compiler_params=params(16),
+        grid=(rows // edge,),
+        in_specs=[pl.BlockSpec((edge, cols), lambda k: (k, 0)), pl.BlockSpec((rank, edge), lambda k: (0, k))],
+        out_specs=(
+            pl.BlockSpec((row_peers, half * rank, cols), lambda k: (0, k, 0)),
+            pl.BlockSpec((edge, cols), lambda k: (0, 0)),
+            pl.BlockSpec((edge, cols), lambda k: (0, 0)),
+        ),
+        compiler_params=params(60),
         cost_estimate=cost(2 * rows * rank * cols, 5 << 20),
         name="coeffs",
     )(panel, col_basis.T)
@@ -176,7 +190,7 @@
 
     info = jnp.stack([blk_count.reshape(()), core.astype(I32)])
     x = jnp.transpose(couplings.reshape(slots, rank, rank), (1, 2, 0)).reshape(rank * rank, slots)
-    ct, table = pl.pallas_call(
+    prep = pl.pallas_call(
         functools.partial(prep_kernel, clusters, rank, groups),
         out_shape=(jax.ShapeDtypeStruct((slots, rank * rank), BF16), jax.ShapeDtypeStruct((8, slots), I32)),
         in_specs=[SMEM, VMEM, VMEM, VMEM],
@@ -184,7 +198,8 @@
         compiler_params=params(24),
         cost_estimate=cost(2 * slots * slots * rank * rank, 1 << 20),
         name="prep",
-    )(info, blk_rows.reshape(1, slots), blk_cols.reshape(1, slots), x)
+    )
+    ct, table = prep(info, blk_rows.reshape(1, slots), blk_cols.reshape(1, slots), x)
 
     mine, theirs = pl.pallas_call(
         functools.partial(block_kernel, rank, 128 // rank, 4),
@@ -211,38 +226,41 @@
         summed.reshape(col_peers // 2, clusters * rank, cols), ("x", "zh"), 0, 0, tiled=True
     )
 
+    held = 2
     near = pl.pallas_call(
         functools.partial(near_kernel, half, leaf),
         out_shape=jax.ShapeDtypeStruct((rows, cols), F32),
-        grid=(clusters,),
+        grid=(clusters // held,),
         in_specs=[
-            pl.BlockSpec((1, near_count, leaf, leaf), lambda k: (k, 0, 0, 0)),
+            pl.BlockSpec((held, near_count, leaf, leaf), lambda k: (k, 0, 0, 0)),
             pl.BlockSpec((rows, cols), lambda k: (0, 0)),
-            pl.BlockSpec((half * leaf, cols), lambda k: (0, 0)),
-            pl.BlockSpec((half * leaf, cols), lambda k: (0, 0)),
+            pl.BlockSpec((edge, cols), lambda k: (0, 0)),
+            pl.BlockSpec((edge, cols), lambda k: (0, 0)),
         ],
-        out_specs=pl.BlockSpec((leaf, cols), lambda k: (k, 0)),
-        scratch_shapes=[pltpu.VMEM((rows + 2 * half * leaf, cols), BF16)],
-        compiler_params=params(32),
+        out_specs=pl.BlockSpec((held * leaf, cols), lambda k: (k, 0)),
+        scratch_shapes=[pltpu.VMEM((rows + 2 * edge, cols), BF16)],
+        compiler_params=params(60),
         cost_estimate=cost(2 * clusters * near_count * leaf * leaf * cols, 28 << 20),
         name="near",
-    )(near_blocks, panel, low, high)
+    )
+    near = near(near_blocks, panel, low, high)
 
     place = lax.axis_index(COL).astype(I32).reshape(1)
+    steps = 4
     return pl.pallas_call(
-        final_kernel,
+        functools.partial(final_kernel, rank, leaf),
         out_shape=jax.ShapeDtypeStruct((rows, cols), BF16),
         grid_spec=pltpu.PrefetchScalarGridSpec(
             num_scalar_prefetch=1,
-            grid=(clusters,),
+            grid=(steps,),
             in_specs=[
-                pl.BlockSpec((col_peers // 2, rank, cols), lambda k, at: (0, k, 0)),
-                pl.BlockSpec((rank, leaf), lambda k, at: (0, at[0] * clusters + k)),
-                pl.BlockSpec((leaf, cols), lambda k, at: (k, 0)),
+                pl.BlockSpec((col_peers // 2, clusters * rank // steps, cols), lambda k, at: (0, k, 0)),
+                pl.BlockSpec((rank, rows // steps), lambda k, at: (0, at[0] * steps + k)),
+                pl.BlockSpec((rows // steps, cols), lambda k, at: (k, 0)),
             ],
-            out_specs=pl.BlockSpec((leaf, cols), lambda k, at: (k, 0)),
+            out_specs=pl.BlockSpec((rows // steps, cols), lambda k, at: (k, 0)),
         ),
-        compiler_params=params(16),
+        compiler_params=params(32),
         cost_estimate=cost(4 * rows * rank * cols, 8 << 20),
         name="final",
     )(place, parts, row_basis.T, near)
@@ -261,6 +279,4 @@
         P(ROW, COL, None),
         P(ROW, COL),
     )
-    return jax.shard_map(
-        on_device, mesh=fine, in_specs=placed, out_specs=P((*ROW, *COL), None), check_vma=False
-    )
+    return jax.shard_map(on_device, mesh=fine, in_specs=placed, out_specs=P((*ROW, *COL), None), check_vma=False)

time: 89.4 us -> 79.3 us (0.89)
  local copies, waits for them, and re-layouts: 9.2 us -> 2.2 us
  Pallas kernels: 30.8 us -> 27.9 us
    unnamed x20 -> x10, local copies, waits for them, and re-layouts: 9.2 us -> 2.2 us
    pallas_call x4, Pallas kernels: 26.5 us -> 22.6 us  [the longest x1 13.6 us: on_device(): near = near(near_blocks, panel, low, high)]
    pallas_call x1, Pallas kernels: 0.24 us -> 1.21 us  [on_device(): pl.pallas_call(pair_kernel, out_shape=jax.ShapeDtypeStruct(mine.shape, BF...]
  transfers between devices with their start and end apart: 5 -> 5, of which waited for: 3 -> 3; matrix products, arithmetic and copies ran while one was open for 0% -> 0% of each run, Pallas kernels for 20% -> 21%
where the time goes in v2:
time: 79.3 us; the launch traced here: 78.9 us
  waiting for transfers between devices  28.8 us (36%)
  Pallas kernels  27.9 us (35%)
  starting transfers between devices  19.3 us (24%)
  local copies, waits for them, and re-layouts  2.2 us (3%)
    ppermute x1, waiting for transfers between devices, on_device(): low = lax.ppermute(tail, every, up)  14.4 us
    pallas_call x1, Pallas kernels, on_device(): near = near(near_blocks, panel, low, high)  13.6 us
    all_to_all x1, waiting for transfers between devices, on_device(): gathered = lax.all_to_all(send, ROW, 0, 0, tiled=True)  11 us
    all_to_all x1, starting transfers between devices, on_device(): gathered = lax.all_to_all(send, ROW, 0, 0, tiled=True)  5.71 us
    ppermute x1, starting transfers between devices, on_device(): low = lax.ppermute(tail, every, up)  5.11 us
    pallas_call x1, Pallas kernels, on_device(): pl.pallas_call(functools.partial(coeff_kernel, row_peers, leaf, rank), ou...  4.38 us
    all_to_all x1, starting transfers between devices, on_device(): lax.all_to_all(summed.reshape(col_peers // 2, clusters * rank, cols), ('x...  4.32 us
    pallas_call x1, Pallas kernels, on_device(): pl.pallas_call(functools.partial(block_kernel, rank, 128 // rank, 4), out...  4.07 us
  transfers between devices with their start and end apart: 5, of which 3 were waited for; matrix products, arithmetic and copies ran while one was open for 0% of the time, Pallas kernels for 21%

profile of v2, /device:TPU:9, one launch (start us, length us, event | category | flops | bytes accessed | tf_op | source)
XLA Modules:
  0.0 78.9 jit_solution(13066873801155319712)
XLA Ops:
  0.0 0.0 copy-start.2
  0.0 0.0 copy-start.3
  0.0 0.0 copy-start.4
  0.0 4.4 %coeffs.1 = (bf16[8,256,256]{2,1,0:T(8,128)(2,1)}, bf16[1024,256]{1,0:T(8,128)(2,1)}, bf16[1024,256]{1,0:T(8,128)(2,1)}) custom-call(bf16[4096,256]{1,0:T(8,128)(2,1)} %panel_ref.3, bf16[16,4096]{1,0:T(8,128)(2,1)} %bitcast.20), custom_call_target="tpu_custom_call" | custom-call | flops 33554432 | bytes 5242880 | tf_op jit(solution)/shard_map/coeffs/pallas_call | solution.py:165
  4.4 5.7 %all-to-all-start = ((bf16[8,256,256]{2,1,0:T(8,128)(2,1)}), bf16[8,256,256]{2,1,0:T(8,128)(2,1)S(1)}, u32[]{:S(2)}, u32[]{:S(2)}) async-start(bf16[8,256,256]{2,1,0:T(8,128)(2,1)} %get-tuple-element.14), calls=%async_computation | async-start | bytes 2097152 | tf_op jit(solution)/shard_map/all_to_all | solution.py:183
  10.7 0.1 pad_add_fusion.info_ref
  10.8 0.0 copy-done.2
  10.8 0.0 copy-done.3
  10.8 0.0 copy-done.4
  10.8 1.9 %prep.1 = (bf16[512,256]{1,0:T(8,128)(2,1)S(1)}, s32[8,512]{1,0:T(8,128)S(1)}) custom-call(s32[2]{0:T(128)S(1)} %pad_add_fusion.info_ref, s32[1,512]{1,0:T(1,128)S(1)} %bitcast.18, s32[1,512]{1,0:T(1,128)S(1)} %bitcast.19, bf16[256,512]{1,0:T(8,128)(2,1)S(1)} %bitcast.17), custom_call_target="tpu_custom_call" | custom-call | flops 134217728 | bytes 1048576 | tf_op jit(solution)/shard_map/prep/pallas_call | solution.py:202
  12.7 11.0 %all-to-all-done = bf16[8,256,256]{2,1,0:T(8,128)(2,1)S(1)} async-done(((bf16[8,256,256]{2,1,0:T(8,128)(2,1)}), bf16[8,256,256]{2,1,0:T(8,128)(2,1)S(1)}, u32[]{:S(2)}, u32[]{:S(2)}) %all-to-all-start) | async-done | bytes 1048608 | tf_op jit(solution)/shard_map/all_to_all | solution.py:183
  23.8 4.1 %blocks.1 = (bf16[2048,256]{1,0:T(8,128)(2,1)S(1)}, bf16[2048,256]{1,0:T(8,128)(2,1)S(1)}) custom-call(s32[8,512]{1,0:T(8,128)S(1)} %get-tuple-element.12.table_ref, bf16[512,256]{1,0:T(8,128)(2,1)S(1)} %get-tuple-element.13.ct_ref, bf16[2048,256]{1,0:T(8,128)(2,1)S(1)} %bitcast.16), custom_call_target="tpu_custom_call" | custom-call | flops 536870912 | bytes 4194304 | tf_op jit(solution)/shard_map/blocks/pallas_call | solution.py:204
  27.8 2.2 %collective-permute-start = (bf16[2048,256]{1,0:T(8,128)(2,1)S(1)}, bf16[2048,256]{1,0:T(8,128)(2,1)S(1)}, u32[]{:S(2)}, u32[]{:S(2)}) collective-permute-start(bf16[2048,256]{1,0:T(8,128)(2,1)S(1)} %get-tuple-element.16), channel_id=1, source_target_pairs={{0,1},{1,0},{2,3},{3,2},{4,5},{5,4},{6,7},{7,6},{8,9},{9,8},{10,11... | collective-permute-start | bytes 3145736 | tf_op jit(solution)/shard_map/ppermute | solution.py:215
  30.0 5.1 %collective-permute-start.1 = (bf16[1024,256]{1,0:T(8,128)(2,1)}, bf16[1024,256]{1,0:T(8,128)(2,1)}, u32[]{:S(2)}, u32[]{:S(2)}) collective-permute-start(bf16[1024,256]{1,0:T(8,128)(2,1)} %get-tuple-element.17), channel_id=1, source_target_pairs={{0,1},{1,2},{2,3},{3,4},{4,5},{5,6},{6,7},{7,8},{8,9},{9,10},{10,1... | collective-permute-start | bytes 1572872 | tf_op jit(solution)/shard_map/ppermute | solution.py:188
  35.1 1.9 %collective-permute-start.2 = (bf16[1024,256]{1,0:T(8,128)(2,1)}, bf16[1024,256]{1,0:T(8,128)(2,1)}, u32[]{:S(2)}, u32[]{:S(2)}) collective-permute-start(bf16[1024,256]{1,0:T(8,128)(2,1)} %get-tuple-element.18), channel_id=1, source_target_pairs={{1,0},{2,1},{3,2},{4,3},{5,4},{6,5},{7,6},{8,7},{9,8},{10,9},{11,1... | collective-permute-start | bytes 1572872 | tf_op jit(solution)/shard_map/ppermute | solution.py:189
  37.1 0.0 collective-permute-done.b_ref
  37.1 1.2 %pair.1 = bf16[2048,256]{1,0:T(8,128)(2,1)} custom-call(bf16[2048,256]{1,0:T(8,128)(2,1)S(1)} %get-tuple-element.15.a_ref, bf16[2048,256]{1,0:T(8,128)(2,1)S(1)} %collective-permute-done.b_ref), custom_call_target="tpu_custom_call" | custom-call | flops 524288 | bytes 3145728 | tf_op jit(solution)/shard_map/pair/pallas_call | solution.py:216
  38.3 4.3 %all-to-all-start.1 = ((bf16[8,256,256]{2,1,0:T(8,128)(2,1)}), bf16[8,256,256]{2,1,0:T(8,128)(2,1)S(1)}, u32[]{:S(2)}, u32[]{:S(2)}) async-start(bf16[8,256,256]{2,1,0:T(8,128)(2,1)} %bitcast.10), calls=%async_computation.1 | async-start | bytes 2097152 | tf_op jit(solution)/shard_map/all_to_all | solution.py:225
  42.6 0.0 copy-start.1
  42.6 14.4 %collective-permute-done.1.low_ref = bf16[1024,256]{1,0:T(8,128)(2,1)} collective-permute-done((bf16[1024,256]{1,0:T(8,128)(2,1)}, bf16[1024,256]{1,0:T(8,128)(2,1)}, u32[]{:S(2)}, u32[]{:S(2)}) %collective-permute-start.1) | collective-permute-done | bytes 524320 | tf_op jit(solution)/shard_map/ppermute | solution.py:188
  57.0 3.4 %collective-permute-done.2.high_ref = bf16[1024,256]{1,0:T(8,128)(2,1)} collective-permute-done((bf16[1024,256]{1,0:T(8,128)(2,1)}, bf16[1024,256]{1,0:T(8,128)(2,1)}, u32[]{:S(2)}, u32[]{:S(2)}) %collective-permute-start.2) | collective-permute-done | bytes 524320 | tf_op jit(solution)/shard_map/ppermute | solution.py:189
  60.4 13.6 %near.1.near_ref = f32[4096,256]{1,0:T(8,128)} custom-call(bf16[16,9,256,256]{3,2,1,0:T(8,128)(2,1)} %nb_ref.1, bf16[4096,256]{1,0:T(8,128)(2,1)} %panel_ref.3, bf16[1024,256]{1,0:T(8,128)(2,1)} %collective-permute-done.1.low_ref, bf16[1024,256]{1,0:T(8,128)(2,1)} %collective-permute-done.2.high_ref), custom_call_target="tpu_custom_call" | custom-call | flops 4831838208 | bytes 29360128 | tf_op jit(solution)/shard_map/near/pallas_call | solution.py:246
  74.0 0.0 all-to-all-done.1.parts_ref
  74.0 0.0 copy-done.1
  74.0 0.0 copy-start
  74.0 2.2 %copy-done = f32[4096,256]{1,0:T(8,128)S(1)} copy-done((f32[4096,256]{1,0:T(8,128)S(1)}, f32[4096,256]{1,0:T(8,128)}, u32[]{:S(2)}) %copy-start) | copy-done | bytes 4194328
  76.2 2.7 %final.1 = bf16[4096,256]{1,0:T(8,128)(2,1)} custom-call(s32[1]{0:T(128)} %bitcast.place_ref, bf16[8,256,256]{2,1,0:T(8,128)(2,1)S(1)} %all-to-all-done.1.parts_ref, bf16[16,65536]{1,0:T(8,128)(2,1)S(1)} %bitcast.15, f32[4096,256]{1,0:T(8,128)S(1)} %copy-done), custom_call_target="tpu_custom_call" | custom-call | flops 67108864 | bytes 8388608 | tf_op jit(solution)/shard_map/final/pallas_call | solution.py:250
Async XLA Ops:
  0.0 10.8 %copy-start.2 = (bf16[1,1,512,16,16]{2,4,3,1,0:T(8,128)(2,1)S(1)}, bf16[1,1,512,16,16]{2,4,3,1,0:T(8,128)(2,1)}, u32[]{:S(2)}) copy-start(bf16[1,1,512,16,16]{2,4,3,1,0:T(8,128)(2,1)} %param.12) | copy-start | bytes 786436
  0.0 10.8 %copy-start.3 = (s32[1,1,512]{2,1,0:T(1,128)S(1)}, s32[1,1,512]{2,1,0:T(1,128)}, u32[]{:S(2)}) copy-start(s32[1,1,512]{2,1,0:T(1,128)} %param.13) | copy-start | bytes 6148
  0.0 10.8 %copy-start.4 = (s32[1,1,512]{2,1,0:T(1,128)S(1)}, s32[1,1,512]{2,1,0:T(1,128)}, u32[]{:S(2)}) copy-start(s32[1,1,512]{2,1,0:T(1,128)} %param.14) | copy-start | bytes 6148
  4.4 19.4 %all-to-all-start = ((bf16[8,256,256]{2,1,0:T(8,128)(2,1)}), bf16[8,256,256]{2,1,0:T(8,128)(2,1)S(1)}, u32[]{:S(2)}, u32[]{:S(2)}) async-start(bf16[8,256,256]{2,1,0:T(8,128)(2,1)} %get-tuple-element.14), calls=%async_computation | async-start | bytes 2097152 | tf_op jit(solution)/shard_map/all_to_all | solution.py:183
  27.8 9.2 %collective-permute-start = (bf16[2048,256]{1,0:T(8,128)(2,1)S(1)}, bf16[2048,256]{1,0:T(8,128)(2,1)S(1)}, u32[]{:S(2)}, u32[]{:S(2)}) collective-permute-start(bf16[2048,256]{1,0:T(8,128)(2,1)S(1)} %get-tuple-element.16), channel_id=1, source_target_pairs={{0,1},{1,0},{2,3},{3,2},{4,5},{5,4},{6,7},{7,6},{8,9},{9,8},{10,11... | collective-permute-start | bytes 3145736 | tf_op jit(solution)/shard_map/ppermute | solution.py:215
  30.0 27.0 %collective-permute-start.1 = (bf16[1024,256]{1,0:T(8,128)(2,1)}, bf16[1024,256]{1,0:T(8,128)(2,1)}, u32[]{:S(2)}, u32[]{:S(2)}) collective-permute-start(bf16[1024,256]{1,0:T(8,128)(2,1)} %get-tuple-element.17), channel_id=1, source_target_pairs={{0,1},{1,2},{2,3},{3,4},{4,5},{5,6},{6,7},{7,8},{8,9},{9,10},{10,1... | collective-permute-start | bytes 1572872 | tf_op jit(solution)/shard_map/ppermute | solution.py:188
  35.1 25.2 %collective-permute-start.2 = (bf16[1024,256]{1,0:T(8,128)(2,1)}, bf16[1024,256]{1,0:T(8,128)(2,1)}, u32[]{:S(2)}, u32[]{:S(2)}) collective-permute-start(bf16[1024,256]{1,0:T(8,128)(2,1)} %get-tuple-element.18), channel_id=1, source_target_pairs={{1,0},{2,1},{3,2},{4,3},{5,4},{6,5},{7,6},{8,7},{9,8},{10,9},{11,1... | collective-permute-start | bytes 1572872 | tf_op jit(solution)/shard_map/ppermute | solution.py:189
  38.3 35.7 %all-to-all-start.1 = ((bf16[8,256,256]{2,1,0:T(8,128)(2,1)}), bf16[8,256,256]{2,1,0:T(8,128)(2,1)S(1)}, u32[]{:S(2)}, u32[]{:S(2)}) async-start(bf16[8,256,256]{2,1,0:T(8,128)(2,1)} %bitcast.10), calls=%async_computation.1 | async-start | bytes 2097152 | tf_op jit(solution)/shard_map/all_to_all | solution.py:225
  42.6 31.4 %copy-start.1 = (bf16[65536,16]{0,1:T(8,128)(2,1)S(1)}, bf16[65536,16]{0,1:T(8,128)(2,1)}, u32[]{:S(2)}) copy-start(bf16[65536,16]{0,1:T(8,128)(2,1)} %param.9) | copy-start | bytes 6291460
  74.0 2.2 %copy-start = (f32[4096,256]{1,0:T(8,128)S(1)}, f32[4096,256]{1,0:T(8,128)}, u32[]{:S(2)}) copy-start(f32[4096,256]{1,0:T(8,128)} %near.1.near_ref) | copy-start | bytes 12582916

commit v3 on v2

v3 whole, which is shorter than its diff:
```python
import functools

import jax
import jax.numpy as jnp
from jax import lax
from jax.experimental import pallas as pl
from jax.experimental.pallas import tpu as pltpu
from jax.sharding import Mesh, PartitionSpec as P


F32, BF16, I32 = jnp.float32, jnp.bfloat16, jnp.int32
ROW, COL = ("zl", "y"), ("x", "zh", "core")
NT = (((1,), (1,)), ((), ()))
TN = (((0,), (0,)), ((), ()))
VMEM = pl.BlockSpec(memory_space=pltpu.VMEM)
SMEM = pl.BlockSpec(memory_space=pltpu.SMEM)
HBM = pl.BlockSpec(memory_space=pltpu.HBM)


def cost(flops, nbytes):
    return pl.CostEstimate(flops=flops, bytes_accessed=nbytes, transcendentals=0)


def params(mib):
    return pltpu.CompilerParams(vmem_limit_bytes=mib << 20)


def coeff_kernel(
    leaf, rank, chunks, core_ref, panel_ref, vt_ref, own_ref, chip_ref, far_ref, panel, vt, in_sem, v_sem, edge_sem
):
    rows = panel.shape[0]
    size, edge = rows // chunks, chip_ref.shape[0]
    load_v = pltpu.make_async_copy(vt_ref, vt, v_sem)
    load_v.start()
    loads = []
    for c in range(chunks):
        span = pl.ds(c * size, size)
        loads.append(pltpu.make_async_copy(panel_ref.at[span], panel.at[span], in_sem.at[c]))
        loads[-1].start()
    load_v.wait()
    for c in range(chunks):
        loads[c].wait()
        for k in range(c * size // leaf, (c + 1) * size // leaf):
            span = pl.ds(k * leaf, leaf)
            own_ref[pl.ds(k * rank, rank), :] = jnp.dot(
                vt[:, span], panel[span, :], preferred_element_type=F32
            ).astype(BF16)
    tail = jnp.where(core_ref[0] == 0, rows - edge, 0)
    head = rows - edge - tail
    stores = [
        pltpu.make_async_copy(panel.at[pl.ds(pl.multiple_of(at, edge), edge)], ref, edge_sem.at[i])
        for i, (at, ref) in enumerate(((tail, chip_ref), (head, far_ref)))
    ]
    for store in stores:
        store.start()
    for store in stores:
        store.wait()


def prep_kernel(per_dev, rank, groups, info_ref, rows_ref, cols_ref, x_ref, ct_ref, table_ref):
    slots = rows_ref.shape[1]
    count, core = info_ref[0], info_ref[1]
    lane = lax.broadcasted_iota(I32, (1, slots), 1)
    live = lane < count
    rows = rows_ref[...]
    dest, local = rows // per_dev, rows % per_dev
    other = jnp.where(dest % 2 == core, 1, 0)
    row_key = other * (groups // 2) + (dest // 2) * per_dev + local
    key = jnp.where(live, row_key, groups) * slots + lane
    down = lax.broadcasted_iota(I32, (slots, slots), 0)
    across = lax.broadcasted_iota(I32, (slots, slots), 1)
    key_down = jnp.sum(jnp.where(down == across, key, 0), axis=1, keepdims=True)
    place = jnp.sum((key_down < key).astype(I32), axis=0, keepdims=True)
    place = jnp.where(live, place, -1)
    pick = (down == place).astype(F32).astype(BF16)
    value = lax.dot_general(pick, x_ref[...], NT, preferred_element_type=F32)
    width = value.shape[1]
    k_of = lax.broadcasted_iota(I32, value.shape, 0)
    i_of = lax.broadcasted_iota(I32, value.shape, 1) // rank
    step = 1
    while step < rank:
        k_bit, i_bit = (k_of // step) % 2, (i_of // step) % 2
        ahead = pltpu.roll(pltpu.roll(value, slots - step, 0), step * rank, 1)
        behind = pltpu.roll(pltpu.roll(value, step, 0), width - step * rank, 1)
        value = jnp.where(k_bit == i_bit, value, jnp.where(k_bit == 0, ahead, behind))
        step *= 2
    ct_ref[...] = value.astype(BF16)
    top = jnp.max(jnp.where(live, row_key, 0))
    cols = cols_ref[...] ^ (info_ref[2] * per_dev)
    pair = jnp.concatenate([cols, row_key] + [jnp.zeros_like(row_key)] * 6, axis=0)
    table = lax.dot_general(pair.astype(F32).astype(BF16), pick, NT, preferred_element_type=F32).astype(I32)
    which = lax.broadcasted_iota(I32, table.shape, 0)
    past = lax.broadcasted_iota(I32, table.shape, 1) >= count
    table_ref[...] = jnp.where(past & (which == 1), top, table)


def block_kernel(rank, tile, unroll, table_ref, ct_ref, *refs):
    *parts, own_ref, other_ref, out_ref, g_ref = refs
    slots = table_ref.shape[1]
    cols = g_ref.shape[1]
    size = parts[0].shape[0]
    for j, part in enumerate(parts):
        g_ref[pl.ds(j * size, size), :] = part[...]
    out_ref[...] = jnp.zeros_like(out_ref)
    width = tile * rank
    group = lax.broadcasted_iota(I32, (rank, width), 1) // rank
    masks = [(group == k).astype(F32).astype(BF16) for k in range(tile)]
    halves = ct_ref.shape[1] // width

    def body(step, carry):
        acc, last = carry
        for u in range(unroll):
            for h in range(halves):
                base = (step * unroll + u) * tile * halves + h * tile
                ct = ct_ref[pl.ds(pl.multiple_of((step * unroll + u) * rank, rank), rank), h * width : (h + 1) * width]
                lhs = jnp.concatenate([ct * m for m in masks], axis=0)
                rhs = jnp.concatenate(
                    [
                        g_ref[pl.ds(pl.multiple_of(table_ref[0, base + k] * rank, rank), rank), :]
                        for k in range(tile)
                    ],
                    axis=0,
                )
                terms = jnp.dot(lhs, rhs, preferred_element_type=F32)
                for k in range(tile):
                    row = table_ref[1, base + k]
                    term = terms[k * rank : (k + 1) * rank, :]
                    acc = term + jnp.where(row == last, acc, 0.0)
                    last = row
                    out_ref[pl.ds(pl.multiple_of(row * rank, rank), rank), :] = acc.astype(BF16)
        return acc, last

    steps = slots // (tile * halves * unroll)
    lax.fori_loop(0, steps, body, (jnp.zeros((rank, cols), F32), jnp.int32(-1)))
    size = own_ref.shape[0]
    other_ref[...] = out_ref[pl.ds(0, size), :]
    own_ref[...] = out_ref[pl.ds(size, size), :]


def pair_kernel(chunks, a_ref, b_ref, out_ref, out, sem):
    size = out.shape[0] // chunks
    stores = []
    for c in range(chunks):
        span = pl.ds(c * size, size)
        out[span, :] = (a_ref[span, :].astype(F32) + b_ref[span, :].astype(F32)).astype(BF16)
        stores.append(pltpu.make_async_copy(out.at[span], out_ref.at[span], sem.at[c]))
        stores[-1].start()
    for store in stores:
        store.wait()


def near_kernel(
    group, core_ref, nb_ref, panel_ref, chip_ref, far_ref, out_ref, window, blocks, out, w_sem, nb_sem, out_sem
):
    clusters, near_count, leaf, _ = nb_ref.shape
    rows, edge = panel_ref.shape[0], chip_ref.shape[0]

    def load(k):
        return pltpu.make_async_copy(nb_ref.at[k], blocks.at[k], nb_sem.at[k])

    def store(p):
        span = pl.ds(pl.multiple_of(p * group * leaf, leaf), group * leaf)
        return pltpu.make_async_copy(out.at[span], out_ref.at[span], out_sem.at[p])

    chip_at = jnp.where(core_ref[0] == 0, edge + rows, 0)
    far_at = edge + rows - chip_at
    fills = [
        pltpu.make_async_copy(ref, window.at[pl.ds(pl.multiple_of(at, leaf), ref.shape[0])], w_sem.at[i])
        for i, (at, ref) in enumerate(((edge, panel_ref), (chip_at, chip_ref), (far_at, far_ref)))
    ]
    for fill in fills:
        fill.start()
    for k in range(clusters):
        load(k).start()
    for fill in fills:
        fill.wait()

    def body(p, carry):
        for c in range(group):
            load(p * group + c).wait()
        for c in range(group):
            k = p * group + c
            lhs = jnp.concatenate([blocks[k, o] for o in range(near_count)], axis=1)
            rhs = window[pl.ds(pl.multiple_of(k * leaf, leaf), near_count * leaf), :]
            out[pl.ds(pl.multiple_of(k * leaf, leaf), leaf), :] = jnp.dot(
                lhs, rhs, preferred_element_type=F32
            ).astype(BF16)
        store(p).start()
        return carry

    lax.fori_loop(0, clusters // group, body, 0)
    for p in range(clusters // group):
        store(p).wait()


def final_kernel(
    rank, leaf, place_ref, parts, ut_ref, near_ref, out_ref,
    ut, near, out, ut_sem, near_sem, out_sem,
):
    rows = out.shape[0]
    chunks = near_sem.shape[0]
    size = rows // chunks
    loads = [pltpu.make_async_copy(ut_ref.at[:, pl.ds(pl.multiple_of(place_ref[0] * rows, rows), rows)], ut, ut_sem)]
    for c in range(chunks):
        span = pl.ds(c * size, size)
        loads.append(pltpu.make_async_copy(near_ref.at[span], near.at[span], near_sem.at[c]))
    for load in loads:
        load.start()
    loads[0].wait()
    stores = []
    for c in range(chunks):
        loads[1 + c].wait()
        for k in range(c * size // leaf, (c + 1) * size // leaf):
            span, ranks = pl.ds(k * leaf, leaf), pl.ds(k * rank, rank)
            coupled = parts[0, ranks, :].astype(F32)
            for p in range(1, parts.shape[0]):
                coupled = coupled + parts[p, ranks, :].astype(F32)
            high = coupled.astype(BF16)
            low = (coupled - high.astype(F32)).astype(BF16)
            both = jnp.concatenate([ut[:, span]] * 2, axis=0)
            far = lax.dot_general(both, jnp.concatenate([high, low], axis=0), TN, preferred_element_type=F32)
            out[span, :] = (near[span, :].astype(F32) + far).astype(BF16)
        span = pl.ds(c * size, size)
        stores.append(pltpu.make_async_copy(out.at[span], out_ref.at[span], out_sem.at[c]))
        stores[-1].start()
    for store in stores:
        store.wait()


def on_device(panel, row_basis, col_basis, near_blocks, couplings, blk_rows, blk_cols, blk_count):
    rows, cols = panel.shape
    clusters, near_count, leaf, _ = near_blocks.shape
    rank, slots = col_basis.shape[1], couplings.shape[2]
    half = near_count // 2
    row_peers, col_peers = lax.axis_size(ROW), lax.axis_size(COL)
    groups = col_peers * clusters
    core = lax.axis_index("core")

    edge = half * leaf
    chunks = 4
    here = core.astype(I32).reshape(1)
    coeffs = pl.pallas_call(
        functools.partial(coeff_kernel, leaf, rank, chunks),
        out_shape=(
            jax.ShapeDtypeStruct((clusters * rank, cols), BF16),
            jax.ShapeDtypeStruct((edge, cols), BF16),
            jax.ShapeDtypeStruct((edge, cols), BF16),
        ),
        in_specs=[SMEM, HBM, HBM],
        out_specs=(VMEM, HBM, HBM),
        scratch_shapes=[
            pltpu.VMEM((rows, cols), BF16),
            pltpu.VMEM((rank, rows), BF16),
            pltpu.SemaphoreType.DMA((chunks,)),
            pltpu.SemaphoreType.DMA,
            pltpu.SemaphoreType.DMA((2,)),
        ],
        compiler_params=params(52),
        cost_estimate=cost(2 * rows * rank * cols, 5 << 20),
        name="coeffs",
    )
    own, to_chip, to_far = coeffs(here, panel, col_basis.T)

    def swap_over(x, axis, bits):
        n = lax.axis_size(axis)
        return lax.ppermute(x, axis, [(i, i ^ bits) for i in range(n)])

    y_peers = lax.axis_size("y")
    order = (1, 3, 2)
    across = swap_over(own, "zl", 1)
    held_rows = {0: own, y_peers: across}
    for bits in order:
        held_rows[bits] = swap_over(own, "y", bits)
    for bits in order:
        held_rows[y_peers + bits] = swap_over(across, "y", bits)
    gathered = [held_rows[j] for j in range(row_peers)]

    every = ROW + COL
    peers = lax.axis_size(every)
    from_chip = swap_over(to_chip, "core", 1)
    pairs = [(i, i + 1) for i in range(1, peers - 1, 2)]
    from_far = lax.ppermute(to_far, every, pairs + [(b, a) for a, b in pairs])

    info = jnp.stack([blk_count.reshape(()), core.astype(I32), lax.axis_index(ROW).astype(I32)])
    x = jnp.transpose(couplings.reshape(slots, rank, rank), (1, 2, 0)).reshape(rank * rank, slots)
    prep = pl.pallas_call(
        functools.partial(prep_kernel, clusters, rank, groups),
        out_shape=(jax.ShapeDtypeStruct((slots, rank * rank), BF16), jax.ShapeDtypeStruct((8, slots), I32)),
        in_specs=[SMEM, VMEM, VMEM, VMEM],
        out_specs=(VMEM, VMEM),
        compiler_params=params(24),
        cost_estimate=cost(2 * slots * slots * rank * rank, 1 << 20),
        name="prep",
    )
    ct, table = prep(info, blk_rows.reshape(1, slots), blk_cols.reshape(1, slots), x)

    half_rows = groups // 2 * rank

    blocks = pl.pallas_call(
        functools.partial(block_kernel, rank, 128 // rank, 4),
        out_shape=[jax.ShapeDtypeStruct((half_rows, cols), BF16)] * 2,
        in_specs=[SMEM] + [VMEM] * (1 + row_peers),
        out_specs=[VMEM, VMEM],
        scratch_shapes=[
            pltpu.VMEM((groups * rank, cols), BF16),
            pltpu.VMEM((row_peers * clusters * rank, cols), BF16),
        ],
        compiler_params=params(24),
        cost_estimate=cost(2 * slots * rank * 128 * cols, 4 << 20),
        name="blocks",
    )
    mine, theirs = blocks(table, ct, *gathered)
    swapped = swap_over(theirs, "core", 1)
    summed = pl.pallas_call(
        functools.partial(pair_kernel, chunks),
        out_shape=jax.ShapeDtypeStruct(mine.shape, BF16),
        in_specs=[VMEM, VMEM],
        out_specs=HBM,
        scratch_shapes=[pltpu.VMEM(mine.shape, BF16), pltpu.SemaphoreType.DMA((chunks,))],
        compiler_params=params(44),
        cost_estimate=cost(mine.size, 3 << 20),
        name="pair",
    )(mine, swapped)
    parts = lax.all_to_all(
        summed.reshape(col_peers // 2, clusters * rank, cols), ("x", "zh"), 0, 0, tiled=True
    )

    group = 2
    near_call = pl.pallas_call(
        functools.partial(near_kernel, group),
        out_shape=jax.ShapeDtypeStruct((rows, cols), BF16),
        in_specs=[SMEM, HBM, HBM, HBM, HBM],
        out_specs=HBM,
        scratch_shapes=[
            pltpu.VMEM((rows + 2 * edge, cols), BF16),
            pltpu.VMEM(near_blocks.shape, BF16),
            pltpu.VMEM((rows, cols), BF16),
            pltpu.SemaphoreType.DMA((3,)),
            pltpu.SemaphoreType.DMA((clusters,)),
            pltpu.SemaphoreType.DMA((clusters // group,)),
        ],
        compiler_params=params(52),
        cost_estimate=cost(2 * clusters * near_count * leaf * leaf * cols, 24 << 20),
        name="near",
    )
    near = near_call(here, near_blocks, panel, from_chip, from_far)

    place = lax.axis_index(COL).astype(I32).reshape(1)
    return pl.pallas_call(
        functools.partial(final_kernel, rank, leaf),
        out_shape=jax.ShapeDtypeStruct((rows, cols), BF16),
        in_specs=[SMEM, VMEM, HBM, HBM],
        out_specs=HBM,
        scratch_shapes=[
            pltpu.VMEM((rank, rows), BF16),
            pltpu.VMEM((rows, cols), BF16),
            pltpu.VMEM((rows, cols), BF16),
            pltpu.SemaphoreType.DMA,
            pltpu.SemaphoreType.DMA((chunks,)),
            pltpu.SemaphoreType.DMA((chunks,)),
        ],
        compiler_params=params(52),
        cost_estimate=cost(4 * rows * rank * cols, 8 << 20),
        name="final",
    )(place, parts, row_basis.T, near)


def solution(mesh):
    devices = mesh.devices.reshape(2, 4, 4, 2, 2)
    fine = Mesh(devices, ("zl", "y", "x", "zh", "core"))
    placed = (
        P((*ROW, *COL), None),
        P(ROW, None),
        P((*ROW, *COL), None),
        P((*ROW, *COL), None, None, None),
        P(ROW, COL, None, None, None),
        P(ROW, COL, None),
        P(ROW, COL, None),
        P(ROW, COL),
    )
    return jax.shard_map(on_device, mesh=fine, in_specs=placed, out_specs=P((*ROW, *COL), None), check_vma=False)
```

time: 79.3 us -> 69 us (0.87)
  the two profiles are of different devices: /device:TPU:9 before, /device:TPU:1 now
where the time goes in v3:
time: 69 us; the launch traced here: 68.8 us
  waiting for transfers between devices  23.5 us (34%)
  Pallas kernels  22.2 us (32%)
  starting transfers between devices  21.3 us (31%)
  local copies, waits for them, and re-layouts  0.94 us (1%)
  between operations  0.74 us (1%)
    ppermute x1, waiting for transfers between devices, on_device(): from_far = lax.ppermute(to_far, every, pairs + [(b, a) for a, b in pairs])  16.4 us
    ppermute x9, starting transfers between devices, swap_over(): return lax.ppermute(x, axis, [(i, i ^ bits) for i in range(n)])  11.7 us
    pallas_call x1, Pallas kernels, on_device(): near = near_call(here, near_blocks, panel, from_chip, from_far)  9.49 us
    ppermute x9, waiting for transfers between devices, swap_over(): return lax.ppermute(x, axis, [(i, i ^ bits) for i in range(n)])  7.13 us
    ppermute x1, starting transfers between devices, on_device(): from_far = lax.ppermute(to_far, every, pairs + [(b, a) for a, b in pairs])  5.5 us
    pallas_call x1, Pallas kernels, on_device(): mine, theirs = blocks(table, ct, *gathered)  4.1 us
    all_to_all x1, starting transfers between devices, on_device(): lax.all_to_all(summed.reshape(col_peers // 2, clusters * rank, cols), ('x...  4.05 us
    pallas_call x1, Pallas kernels, on_device(): pl.pallas_call(functools.partial(final_kernel, rank, leaf), out_shape=jax...  3.55 us
  transfers between devices with their start and end apart: 11, of which 4 were waited for; matrix products, arithmetic and copies ran while one was open for 0% of the time, Pallas kernels for 18%

profile of v3, /device:TPU:1, one launch (start us, length us, event | category | flops | bytes accessed | tf_op | source)
XLA Modules:
  0.0 68.8 jit_solution(436164844878208988)
XLA Ops:
  0.0 0.0 copy-start.2
  0.0 0.0 copy-start.3
  0.0 0.0 copy-start
  0.0 0.9 %copy-done = bf16[4096,16]{0,1:T(8,128)(2,1)S(1)} copy-done((bf16[4096,16]{0,1:T(8,128)(2,1)S(1)}, bf16[4096,16]{0,1:T(8,128)(2,1)}, u32[]{:S(2)}) %copy-start) | copy-done | bytes 131096
  0.9 0.0 copy-start.1
  0.9 2.1 %coeffs.1 = (bf16[256,256]{1,0:T(8,128)(2,1)S(1)}, bf16[1024,256]{1,0:T(8,128)(2,1)S(1)}, bf16[1024,256]{1,0:T(8,128)(2,1)S(1)}) custom-call(s32[1]{0:T(128)} %bitcast.2.core_ref, bf16[4096,256]{1,0:T(8,128)(2,1)} %panel_ref.3, bf16[16,4096]{1,0:T(8,128)(2,1)S(1)} %bitcast.15), custom_call_target="tpu_custom_call" | custom-call | flops 33554432 | bytes 5242880 | tf_op jit(solution)/shard_map/coeffs/pallas_call | solution.py:262
  3.0 2.5 %collective-permute-start.3 = (bf16[256,256]{1,0:T(8,128)(2,1)S(1)}, bf16[256,256]{1,0:T(8,128)(2,1)S(1)}, u32[]{:S(2)}, u32[]{:S(2)}) collective-permute-start(bf16[256,256]{1,0:T(8,128)(2,1)S(1)} %get-tuple-element.14.refs_0_), channel_id=1, source_target_pairs={{0,64},{64,0},{1,65},{65,1},{2,66},{66,2},{3,67},{67,3},{4,68},{68... | collective-permute-start | bytes 393224 | tf_op jit(solution)/shard_map/ppermute | solution.py:266
  5.5 1.3 %collective-permute-start = (bf16[256,256]{1,0:T(8,128)(2,1)S(1)}, bf16[256,256]{1,0:T(8,128)(2,1)S(1)}, u32[]{:S(2)}, u32[]{:S(2)}) collective-permute-start(bf16[256,256]{1,0:T(8,128)(2,1)S(1)} %get-tuple-element.14.refs_0_), channel_id=1, source_target_pairs={{0,16},{16,0},{32,48},{48,32},{1,17},{17,1},{33,49},{49,33},{2,18}... | collective-permute-start | bytes 393224 | tf_op jit(solution)/shard_map/ppermute | solution.py:266
  6.8 2.6 %collective-permute-start.1 = (bf16[256,256]{1,0:T(8,128)(2,1)S(1)}, bf16[256,256]{1,0:T(8,128)(2,1)S(1)}, u32[]{:S(2)}, u32[]{:S(2)}) collective-permute-start(bf16[256,256]{1,0:T(8,128)(2,1)S(1)} %get-tuple-element.14.refs_0_), channel_id=1, source_target_pairs={{0,32},{16,48},{32,0},{48,16},{1,33},{17,49},{33,1},{49,17},{2,34}... | collective-permute-start | bytes 393224 | tf_op jit(solution)/shard_map/ppermute | solution.py:266
  9.5 0.0 collective-permute-start.2
  9.5 0.0 collective-permute-done.3.refs_4_
  9.5 0.5 collective-permute-start.4
  9.9 3.4 %collective-permute-start.5 = (bf16[256,256]{1,0:T(8,128)(2,1)S(1)}, bf16[256,256]{1,0:T(8,128)(2,1)S(1)}, u32[]{:S(2)}, u32[]{:S(2)}) collective-permute-start(bf16[256,256]{1,0:T(8,128)(2,1)S(1)} %collective-permute-done.3.refs_4_), channel_id=1, source_target_pairs={{0,32},{16,48},{32,0},{48,16},{1,33},{17,49},{33,1},{49,17},{2,34}... | collective-permute-start | bytes 393224 | tf_op jit(solution)/shard_map/ppermute | solution.py:266
  13.3 0.0 collective-permute-done.refs_1_
  13.3 0.0 collective-permute-start.6
  14.0 0.1 pad_add_fusion.info_ref
  14.1 0.0 copy-done.2
  14.1 0.0 copy-done.3
  14.1 0.0 copy-done.1
  14.1 1.9 %prep.1 = (bf16[512,256]{1,0:T(8,128)(2,1)S(1)}, s32[8,512]{1,0:T(8,128)S(1)}) custom-call(s32[3]{0:T(128)S(1)} %pad_add_fusion.info_ref, s32[1,512]{1,0:T(1,128)S(1)} %bitcast.17, s32[1,512]{1,0:T(1,128)S(1)} %bitcast.18, bf16[256,512]{1,0:T(8,128)(2,1)S(1)} %bitcast.16), custom_call_target="tpu_custom_call" | custom-call | flops 134217728 | bytes 1048576 | tf_op jit(solution)/shard_map/prep/pallas_call | solution.py:295
  16.0 0.0 collective-permute-done.1.refs_2_
  16.0 1.0 %collective-permute-done.2.refs_3_ = bf16[256,256]{1,0:T(8,128)(2,1)S(1)} collective-permute-done((bf16[256,256]{1,0:T(8,128)(2,1)S(1)}, bf16[256,256]{1,0:T(8,128)(2,1)S(1)}, u32[]{:S(2)}, u32[]{:S(2)}) %collective-permute-start.2) | collective-permute-done | bytes 131104 | tf_op jit(solution)/shard_map/ppermute | solution.py:266
  17.0 0.0 collective-permute-done.4.refs_5_
  17.0 3.2 %collective-permute-done.5.refs_6_ = bf16[256,256]{1,0:T(8,128)(2,1)S(1)} collective-permute-done((bf16[256,256]{1,0:T(8,128)(2,1)S(1)}, bf16[256,256]{1,0:T(8,128)(2,1)S(1)}, u32[]{:S(2)}, u32[]{:S(2)}) %collective-permute-start.5) | collective-permute-done | bytes 131104 | tf_op jit(solution)/shard_map/ppermute | solution.py:266
  20.2 2.9 %collective-permute-done.6.refs_7_ = bf16[256,256]{1,0:T(8,128)(2,1)S(1)} collective-permute-done((bf16[256,256]{1,0:T(8,128)(2,1)S(1)}, bf16[256,256]{1,0:T(8,128)(2,1)S(1)}, u32[]{:S(2)}, u32[]{:S(2)}) %collective-permute-start.6) | collective-permute-done | bytes 131104 | tf_op jit(solution)/shard_map/ppermute | solution.py:266
  23.1 4.1 %blocks.1 = (bf16[2048,256]{1,0:T(8,128)(2,1)S(1)}, bf16[2048,256]{1,0:T(8,128)(2,1)S(1)}) custom-call(s32[8,512]{1,0:T(8,128)S(1)} %get-tuple-element.12.table_ref, bf16[512,256]{1,0:T(8,128)(2,1)S(1)} %get-tuple-element.13.ct_ref, bf16[256,256]{1,0:T(8,128)(2,1)S(1)} %get-tuple-element.14.refs_0_, bf16[256,256]{1,0:T(8,128)(2,1)S(1)} %collective-permute-done.refs_1_, ...), custom_call_target="tpu_custom_call" | custom-call | flops 536870912 | bytes 4194304 | tf_op jit(solution)/shard_map/blocks/pallas_call | solution.py:312
  27.2 1.3 %collective-permute-start.7 = (bf16[2048,256]{1,0:T(8,128)(2,1)S(1)}, bf16[2048,256]{1,0:T(8,128)(2,1)S(1)}, u32[]{:S(2)}, u32[]{:S(2)}) collective-permute-start(bf16[2048,256]{1,0:T(8,128)(2,1)S(1)} %get-tuple-element.16), channel_id=1, source_target_pairs={{0,1},{1,0},{2,3},{3,2},{4,5},{5,4},{6,7},{7,6},{8,9},{9,8},{10,11... | collective-permute-start | bytes 3145736 | tf_op jit(solution)/shard_map/ppermute | solution.py:266
  28.6 0.1 collective-permute-start.8
  28.6 5.5 %collective-permute-start.9 = (bf16[1024,256]{1,0:T(8,128)(2,1)S(1)}, bf16[1024,256]{1,0:T(8,128)(2,1)S(1)}, u32[]{:S(2)}, u32[]{:S(2)}) collective-permute-start(bf16[1024,256]{1,0:T(8,128)(2,1)S(1)} %get-tuple-element.18), channel_id=1, source_target_pairs={{1,2},{3,4},{5,6},{7,8},{9,10},{11,12},{13,14},{15,16},{17,18},{19... | collective-permute-start | bytes 1572872 | tf_op jit(solution)/shard_map/ppermute | solution.py:282
  34.2 0.0 collective-permute-done.7.b_ref
  34.2 1.1 %pair.1 = bf16[2048,256]{1,0:T(8,128)(2,1)} custom-call(bf16[2048,256]{1,0:T(8,128)(2,1)S(1)} %get-tuple-element.15.a_ref, bf16[2048,256]{1,0:T(8,128)(2,1)S(1)} %collective-permute-done.7.b_ref), custom_call_target="tpu_custom_call" | custom-call | flops 524288 | bytes 3145728 | tf_op jit(solution)/shard_map/pair/pallas_call | solution.py:314
  35.2 4.0 %all-to-all-start = ((bf16[8,256,256]{2,1,0:T(8,128)(2,1)}), bf16[8,256,256]{2,1,0:T(8,128)(2,1)S(1)}, u32[]{:S(2)}, u32[]{:S(2)}) async-start(bf16[8,256,256]{2,1,0:T(8,128)(2,1)} %bitcast.10), calls=%async_computation | async-start | bytes 2097152 | tf_op jit(solution)/shard_map/all_to_all | solution.py:324
  39.3 0.0 collective-permute-done.8.chip_ref
  39.3 16.4 %collective-permute-done.9.far_ref = bf16[1024,256]{1,0:T(8,128)(2,1)S(1)} collective-permute-done((bf16[1024,256]{1,0:T(8,128)(2,1)S(1)}, bf16[1024,256]{1,0:T(8,128)(2,1)S(1)}, u32[]{:S(2)}, u32[]{:S(2)}) %collective-permute-start.9) | collective-permute-done | bytes 524320 | tf_op jit(solution)/shard_map/ppermute | solution.py:282
  55.7 9.5 %near.1.near_ref = bf16[4096,256]{1,0:T(8,128)(2,1)} custom-call(s32[1]{0:T(128)} %bitcast.2.core_ref, bf16[16,9,256,256]{3,2,1,0:T(8,128)(2,1)} %nb_ref.1, bf16[4096,256]{1,0:T(8,128)(2,1)} %panel_ref.3, bf16[1024,256]{1,0:T(8,128)(2,1)S(1)} %collective-permute-done.8.chip_ref, bf16[1024,256]{1,0:T(8,128)(2,1)S(1)} %collective-permute-done.9.far_ref), custom_call_target="tpu_custom_call" | custom-call | flops 4831838208 | bytes 25165824 | tf_op jit(solution)/shard_map/near/pallas_call | solution.py:346
  65.2 0.0 all-to-all-done.parts
  65.2 3.6 %final.1 = bf16[4096,256]{1,0:T(8,128)(2,1)} custom-call(s32[1]{0:T(128)} %bitcast.place_ref, bf16[8,256,256]{2,1,0:T(8,128)(2,1)S(1)} %all-to-all-done.parts, bf16[16,65536]{1,0:T(8,128)(2,1)} %bitcast.19, bf16[4096,256]{1,0:T(8,128)(2,1)} %near.1.near_ref), custom_call_target="tpu_custom_call" | custom-call | flops 67108864 | bytes 8388608 | tf_op jit(solution)/shard_map/final/pallas_call | solution.py:349
Async XLA Ops:
  0.0 14.1 %copy-start.2 = (s32[1,1,512]{2,1,0:T(1,128)S(1)}, s32[1,1,512]{2,1,0:T(1,128)}, u32[]{:S(2)}) copy-start(s32[1,1,512]{2,1,0:T(1,128)} %param.13) | copy-start | bytes 6148
  0.0 14.1 %copy-start.3 = (s32[1,1,512]{2,1,0:T(1,128)S(1)}, s32[1,1,512]{2,1,0:T(1,128)}, u32[]{:S(2)}) copy-start(s32[1,1,512]{2,1,0:T(1,128)} %param.14) | copy-start | bytes 6148
  0.0 0.9 %copy-start = (bf16[4096,16]{0,1:T(8,128)(2,1)S(1)}, bf16[4096,16]{0,1:T(8,128)(2,1)}, u32[]{:S(2)}) copy-start(bf16[4096,16]{0,1:T(8,128)(2,1)} %param.10) | copy-start | bytes 393220
  0.9 13.1 %copy-start.1 = (bf16[1,1,512,16,16]{2,4,3,1,0:T(8,128)(2,1)S(1)}, bf16[1,1,512,16,16]{2,4,3,1,0:T(8,128)(2,1)}, u32[]{:S(2)}) copy-start(bf16[1,1,512,16,16]{2,4,3,1,0:T(8,128)(2,1)} %param.12) | copy-start | bytes 786436
  3.0 6.5 %collective-permute-start.3 = (bf16[256,256]{1,0:T(8,128)(2,1)S(1)}, bf16[256,256]{1,0:T(8,128)(2,1)S(1)}, u32[]{:S(2)}, u32[]{:S(2)}) collective-permute-start(bf16[256,256]{1,0:T(8,128)(2,1)S(1)} %get-tuple-element.14.refs_0_), channel_id=1, source_target_pairs={{0,64},{64,0},{1,65},{65,1},{2,66},{66,2},{3,67},{67,3},{4,68},{68... | collective-permute-start | bytes 393224 | tf_op jit(solution)/shard_map/ppermute | solution.py:266
  5.5 7.8 %collective-permute-start = (bf16[256,256]{1,0:T(8,128)(2,1)S(1)}, bf16[256,256]{1,0:T(8,128)(2,1)S(1)}, u32[]{:S(2)}, u32[]{:S(2)}) collective-permute-start(bf16[256,256]{1,0:T(8,128)(2,1)S(1)} %get-tuple-element.14.refs_0_), channel_id=1, source_target_pairs={{0,16},{16,0},{32,48},{48,32},{1,17},{17,1},{33,49},{49,33},{2,18}... | collective-permute-start | bytes 393224 | tf_op jit(solution)/shard_map/ppermute | solution.py:266
  6.8 9.1 %collective-permute-start.1 = (bf16[256,256]{1,0:T(8,128)(2,1)S(1)}, bf16[256,256]{1,0:T(8,128)(2,1)S(1)}, u32[]{:S(2)}, u32[]{:S(2)}) collective-permute-start(bf16[256,256]{1,0:T(8,128)(2,1)S(1)} %get-tuple-element.14.refs_0_), channel_id=1, source_target_pairs={{0,32},{16,48},{32,0},{48,16},{1,33},{17,49},{33,1},{49,17},{2,34}... | collective-permute-start | bytes 393224 | tf_op jit(solution)/shard_map/ppermute | solution.py:266
  9.5 7.5 %collective-permute-start.2 = (bf16[256,256]{1,0:T(8,128)(2,1)S(1)}, bf16[256,256]{1,0:T(8,128)(2,1)S(1)}, u32[]{:S(2)}, u32[]{:S(2)}) collective-permute-start(bf16[256,256]{1,0:T(8,128)(2,1)S(1)} %get-tuple-element.14.refs_0_), channel_id=1, source_target_pairs={{0,48},{16,32},{32,16},{48,0},{1,49},{17,33},{33,17},{49,1},{2,50}... | collective-permute-start | bytes 393224 | tf_op jit(solution)/shard_map/ppermute | solution.py:266
  9.5 7.5 %collective-permute-start.4 = (bf16[256,256]{1,0:T(8,128)(2,1)S(1)}, bf16[256,256]{1,0:T(8,128)(2,1)S(1)}, u32[]{:S(2)}, u32[]{:S(2)}) collective-permute-start(bf16[256,256]{1,0:T(8,128)(2,1)S(1)} %collective-permute-done.3.refs_4_), channel_id=1, source_target_pairs={{0,16},{16,0},{32,48},{48,32},{1,17},{17,1},{33,49},{49,33},{2,18}... | collective-permute-start | bytes 393224 | tf_op jit(solution)/shard_map/ppermute | solution.py:266
  9.9 10.3 %collective-permute-start.5 = (bf16[256,256]{1,0:T(8,128)(2,1)S(1)}, bf16[256,256]{1,0:T(8,128)(2,1)S(1)}, u32[]{:S(2)}, u32[]{:S(2)}) collective-permute-start(bf16[256,256]{1,0:T(8,128)(2,1)S(1)} %collective-permute-done.3.refs_4_), channel_id=1, source_target_pairs={{0,32},{16,48},{32,0},{48,16},{1,33},{17,49},{33,1},{49,17},{2,34}... | collective-permute-start | bytes 393224 | tf_op jit(solution)/shard_map/ppermute | solution.py:266
  13.3 9.8 %collective-permute-start.6 = (bf16[256,256]{1,0:T(8,128)(2,1)S(1)}, bf16[256,256]{1,0:T(8,128)(2,1)S(1)}, u32[]{:S(2)}, u32[]{:S(2)}) collective-permute-start(bf16[256,256]{1,0:T(8,128)(2,1)S(1)} %collective-permute-done.3.refs_4_), channel_id=1, source_target_pairs={{0,48},{16,32},{32,16},{48,0},{1,49},{17,33},{33,17},{49,1},{2,50}... | collective-permute-start | bytes 393224 | tf_op jit(solution)/shard_map/ppermute | solution.py:266
  27.2 6.9 %collective-permute-start.7 = (bf16[2048,256]{1,0:T(8,128)(2,1)S(1)}, bf16[2048,256]{1,0:T(8,128)(2,1)S(1)}, u32[]{:S(2)}, u32[]{:S(2)}) collective-permute-start(bf16[2048,256]{1,0:T(8,128)(2,1)S(1)} %get-tuple-element.16), channel_id=1, source_target_pairs={{0,1},{1,0},{2,3},{3,2},{4,5},{5,4},{6,7},{7,6},{8,9},{9,8},{10,11... | collective-permute-start | bytes 3145736 | tf_op jit(solution)/shard_map/ppermute | solution.py:266
  28.6 10.7 %collective-permute-start.8 = (bf16[1024,256]{1,0:T(8,128)(2,1)S(1)}, bf16[1024,256]{1,0:T(8,128)(2,1)S(1)}, u32[]{:S(2)}, u32[]{:S(2)}) collective-permute-start(bf16[1024,256]{1,0:T(8,128)(2,1)S(1)} %get-tuple-element.17), channel_id=1, source_target_pairs={{0,1},{1,0},{2,3},{3,2},{4,5},{5,4},{6,7},{7,6},{8,9},{9,8},{10,11... | collective-permute-start | bytes 1572872 | tf_op jit(solution)/shard_map/ppermute | solution.py:266
  28.6 27.1 %collective-permute-start.9 = (bf16[1024,256]{1,0:T(8,128)(2,1)S(1)}, bf16[1024,256]{1,0:T(8,128)(2,1)S(1)}, u32[]{:S(2)}, u32[]{:S(2)}) collective-permute-start(bf16[1024,256]{1,0:T(8,128)(2,1)S(1)} %get-tuple-element.18), channel_id=1, source_target_pairs={{1,2},{3,4},{5,6},{7,8},{9,10},{11,12},{13,14},{15,16},{17,18},{19... | collective-permute-start | bytes 1572872 | tf_op jit(solution)/shard_map/ppermute | solution.py:282
  35.2 30.0 %all-to-all-start = ((bf16[8,256,256]{2,1,0:T(8,128)(2,1)}), bf16[8,256,256]{2,1,0:T(8,128)(2,1)S(1)}, u32[]{:S(2)}, u32[]{:S(2)}) async-start(bf16[8,256,256]{2,1,0:T(8,128)(2,1)} %bitcast.10), calls=%async_computation | async-start | bytes 2097152 | tf_op jit(solution)/shard_map/all_to_all | solution.py:324

commit v4 on v3

--- a/solution.py
+++ b/solution.py
@@ -86,33 +86,41 @@
         step *= 2
     ct_ref[...] = value.astype(BF16)
     top = jnp.max(jnp.where(live, row_key, 0))
+    ahead = jnp.sum((live & (row_key < groups // 2)).astype(I32))
     cols = cols_ref[...] ^ (info_ref[2] * per_dev)
     pair = jnp.concatenate([cols, row_key] + [jnp.zeros_like(row_key)] * 6, axis=0)
     table = lax.dot_general(pair.astype(F32).astype(BF16), pick, NT, preferred_element_type=F32).astype(I32)
     which = lax.broadcasted_iota(I32, table.shape, 0)
     past = lax.broadcasted_iota(I32, table.shape, 1) >= count
-    table_ref[...] = jnp.where(past & (which == 1), top, table)
-
-
-def block_kernel(rank, tile, unroll, table_ref, ct_ref, *refs):
-    *parts, own_ref, other_ref, out_ref, g_ref = refs
-    slots = table_ref.shape[1]
+    table = jnp.where(past & (which == 1), top, table)
+    table_ref[...] = jnp.where(which == 2, ahead, jnp.where(which == 3, count, table))
+
+
+def block_kernel(rank, tile, unroll, second, table_ref, ct_ref, *refs):
+    *parts, out_ref = refs
+    if second:
+        (g_ref,) = parts
+    else:
+        *parts, out_ref, g_ref = refs
+        size = parts[0].shape[0]
+        for j, part in enumerate(parts):
+            g_ref[pl.ds(j * size, size), :] = part[...]
     cols = g_ref.shape[1]
-    size = parts[0].shape[0]
-    for j, part in enumerate(parts):
-        g_ref[pl.ds(j * size, size), :] = part[...]
+    held = out_ref.shape[0] // rank - 1
     out_ref[...] = jnp.zeros_like(out_ref)
     width = tile * rank
     group = lax.broadcasted_iota(I32, (rank, width), 1) // rank
     masks = [(group == k).astype(F32).astype(BF16) for k in range(tile)]
     halves = ct_ref.shape[1] // width
+    per_step = tile * halves * unroll
 
     def body(step, carry):
         acc, last = carry
         for u in range(unroll):
+            at = pl.multiple_of((step * unroll + u) * rank, rank)
             for h in range(halves):
-                base = (step * unroll + u) * tile * halves + h * tile
-                ct = ct_ref[pl.ds(pl.multiple_of((step * unroll + u) * rank, rank), rank), h * width : (h + 1) * width]
+                base = step * per_step + (u * halves + h) * tile
+                ct = ct_ref[pl.ds(at, rank), h * width : (h + 1) * width]
                 lhs = jnp.concatenate([ct * m for m in masks], axis=0)
                 rhs = jnp.concatenate(
                     [
@@ -127,14 +135,16 @@
                     term = terms[k * rank : (k + 1) * rank, :]
                     acc = term + jnp.where(row == last, acc, 0.0)
                     last = row
-                    out_ref[pl.ds(pl.multiple_of(row * rank, rank), rank), :] = acc.astype(BF16)
+                    spot = row - held if second else row
+                    inside = spot >= 0 if second else spot < held
+                    spot = jnp.where(inside, spot, held)
+                    out_ref[pl.ds(pl.multiple_of(spot * rank, rank), rank), :] = acc.astype(BF16)
         return acc, last
 
-    steps = slots // (tile * halves * unroll)
-    lax.fori_loop(0, steps, body, (jnp.zeros((rank, cols), F32), jnp.int32(-1)))
-    size = own_ref.shape[0]
-    other_ref[...] = out_ref[pl.ds(0, size), :]
-    own_ref[...] = out_ref[pl.ds(size, size), :]
+    ahead, count = table_ref[2, 0], table_ref[3, 0]
+    first = ahead // per_step if second else 0
+    end = ((count if second else ahead) + per_step - 1) // per_step
+    lax.fori_loop(first, end, body, (jnp.zeros((rank, cols), F32), jnp.int32(-1)))
 
 
 def pair_kernel(chunks, a_ref, b_ref, out_ref, out, sem):
@@ -296,27 +306,29 @@
 
     half_rows = groups // 2 * rank
 
-    blocks = pl.pallas_call(
-        functools.partial(block_kernel, rank, 128 // rank, 4),
-        out_shape=[jax.ShapeDtypeStruct((half_rows, cols), BF16)] * 2,
-        in_specs=[SMEM] + [VMEM] * (1 + row_peers),
-        out_specs=[VMEM, VMEM],
-        scratch_shapes=[
-            pltpu.VMEM((groups * rank, cols), BF16),
-            pltpu.VMEM((row_peers * clusters * rank, cols), BF16),
-        ],
-        compiler_params=params(24),
-        cost_estimate=cost(2 * slots * rank * 128 * cols, 4 << 20),
-        name="blocks",
-    )
-    mine, theirs = blocks(table, ct, *gathered)
+    kept = jax.ShapeDtypeStruct((half_rows + rank, cols), BF16)
+
+    def blocks(second):
+        held_shape = jax.ShapeDtypeStruct((row_peers * clusters * rank, cols), BF16)
+        return pl.pallas_call(
+            functools.partial(block_kernel, rank, 128 // rank, 2, second),
+            out_shape=kept if second else (kept, held_shape),
+            in_specs=[SMEM] + [VMEM] * (2 if second else 1 + row_peers),
+            out_specs=VMEM if second else (VMEM, VMEM),
+            compiler_params=params(24),
+            cost_estimate=cost(slots * rank * 128 * cols, 2 << 20),
+            name="blocks_own" if second else "blocks_other",
+        )
+
+    theirs, held_all = blocks(False)(table, ct, *gathered)
     swapped = swap_over(theirs, "core", 1)
+    mine = blocks(True)(table, ct, held_all)
     summed = pl.pallas_call(
         functools.partial(pair_kernel, chunks),
-        out_shape=jax.ShapeDtypeStruct(mine.shape, BF16),
+        out_shape=jax.ShapeDtypeStruct((half_rows, cols), BF16),
         in_specs=[VMEM, VMEM],
         out_specs=HBM,
-        scratch_shapes=[pltpu.VMEM(mine.shape, BF16), pltpu.SemaphoreType.DMA((chunks,))],
+        scratch_shapes=[pltpu.VMEM((half_rows, cols), BF16), pltpu.SemaphoreType.DMA((chunks,))],
         compiler_params=params(44),
         cost_estimate=cost(mine.size, 3 << 20),
         name="pair",

time: 69 us -> 66 us (0.957)
  the two profiles are of different devices: /device:TPU:1 before, /device:TPU:5 now
where the time goes in v4:
time: 66 us; the launch traced here: 65.8 us
  starting transfers between devices  22.4 us (34%)
  Pallas kernels  20.8 us (32%)
  waiting for transfers between devices  20.8 us (32%)
  local copies, waits for them, and re-layouts  0.94 us (1%)
  between operations  0.75 us (1%)
    ppermute x1, waiting for transfers between devices, on_device(): from_far = lax.ppermute(to_far, every, pairs + [(b, a) for a, b in pairs])  13.7 us
    ppermute x9, starting transfers between devices, swap_over(): return lax.ppermute(x, axis, [(i, i ^ bits) for i in range(n)])  10.9 us
    pallas_call x1, Pallas kernels, on_device(): near = near_call(here, near_blocks, panel, from_chip, from_far)  9.49 us
    ppermute x9, waiting for transfers between devices, swap_over(): return lax.ppermute(x, axis, [(i, i ^ bits) for i in range(n)])  7.15 us
    ppermute x1, starting transfers between devices, on_device(): from_far = lax.ppermute(to_far, every, pairs + [(b, a) for a, b in pairs])  5.99 us
    all_to_all x1, starting transfers between devices, on_device(): lax.all_to_all(summed.reshape(col_peers // 2, clusters * rank, cols), ('x...  5.44 us
    pallas_call x1, Pallas kernels, on_device(): pl.pallas_call(functools.partial(final_kernel, rank, leaf), out_shape=jax...  3.55 us
    pallas_call x1, Pallas kernels, on_device(): own, to_chip, to_far = coeffs(here, panel, col_basis.T)  2.06 us
  transfers between devices with their start and end apart: 11, of which 4 were waited for; matrix products, arithmetic and copies ran while one was open for 0% of the time, Pallas kernels for 21%

profile of v4, /device:TPU:5, one launch (start us, length us, event | category | flops | bytes accessed | tf_op | source)
XLA Modules:
  0.0 65.8 jit_solution(7116666820597878234)
XLA Ops:
  0.0 0.0 copy-start.2
  0.0 0.0 copy-start.3
  0.0 0.0 copy-start
  0.0 0.9 %copy-done = bf16[4096,16]{0,1:T(8,128)(2,1)S(1)} copy-done((bf16[4096,16]{0,1:T(8,128)(2,1)S(1)}, bf16[4096,16]{0,1:T(8,128)(2,1)}, u32[]{:S(2)}) %copy-start) | copy-done | bytes 131096
  0.9 0.0 copy-start.1
  0.9 2.1 %coeffs.1 = (bf16[256,256]{1,0:T(8,128)(2,1)S(1)}, bf16[1024,256]{1,0:T(8,128)(2,1)S(1)}, bf16[1024,256]{1,0:T(8,128)(2,1)S(1)}) custom-call(s32[1]{0:T(128)} %bitcast.2.core_ref, bf16[4096,256]{1,0:T(8,128)(2,1)} %panel_ref.3, bf16[16,4096]{1,0:T(8,128)(2,1)S(1)} %bitcast.15), custom_call_target="tpu_custom_call" | custom-call | flops 33554432 | bytes 5242880 | tf_op jit(solution)/shard_map/coeffs/pallas_call | solution.py:272
  3.0 1.7 %collective-permute-start.3 = (bf16[256,256]{1,0:T(8,128)(2,1)S(1)}, bf16[256,256]{1,0:T(8,128)(2,1)S(1)}, u32[]{:S(2)}, u32[]{:S(2)}) collective-permute-start(bf16[256,256]{1,0:T(8,128)(2,1)S(1)} %get-tuple-element.14.refs_0_), channel_id=1, source_target_pairs={{0,64},{64,0},{1,65},{65,1},{2,66},{66,2},{3,67},{67,3},{4,68},{68... | collective-permute-start | bytes 393224 | tf_op jit(solution)/shard_map/ppermute | solution.py:276
  4.7 1.3 %collective-permute-start = (bf16[256,256]{1,0:T(8,128)(2,1)S(1)}, bf16[256,256]{1,0:T(8,128)(2,1)S(1)}, u32[]{:S(2)}, u32[]{:S(2)}) collective-permute-start(bf16[256,256]{1,0:T(8,128)(2,1)S(1)} %get-tuple-element.14.refs_0_), channel_id=1, source_target_pairs={{0,16},{16,0},{32,48},{48,32},{1,17},{17,1},{33,49},{49,33},{2,18}... | collective-permute-start | bytes 393224 | tf_op jit(solution)/shard_map/ppermute | solution.py:276
  6.0 2.6 %collective-permute-start.1 = (bf16[256,256]{1,0:T(8,128)(2,1)S(1)}, bf16[256,256]{1,0:T(8,128)(2,1)S(1)}, u32[]{:S(2)}, u32[]{:S(2)}) collective-permute-start(bf16[256,256]{1,0:T(8,128)(2,1)S(1)} %get-tuple-element.14.refs_0_), channel_id=1, source_target_pairs={{0,32},{16,48},{32,0},{48,16},{1,33},{17,49},{33,1},{49,17},{2,34}... | collective-permute-start | bytes 393224 | tf_op jit(solution)/shard_map/ppermute | solution.py:276
  8.6 0.0 collective-permute-start.2
  8.6 0.0 collective-permute-done.3.refs_4_
  8.6 0.5 collective-permute-start.4
  9.1 3.4 %collective-permute-start.5 = (bf16[256,256]{1,0:T(8,128)(2,1)S(1)}, bf16[256,256]{1,0:T(8,128)(2,1)S(1)}, u32[]{:S(2)}, u32[]{:S(2)}) collective-permute-start(bf16[256,256]{1,0:T(8,128)(2,1)S(1)} %collective-permute-done.3.refs_4_), channel_id=1, source_target_pairs={{0,32},{16,48},{32,0},{48,16},{1,33},{17,49},{33,1},{49,17},{2,34}... | collective-permute-start | bytes 393224 | tf_op jit(solution)/shard_map/ppermute | solution.py:276
  12.5 0.0 collective-permute-done.refs_1_
  12.5 0.0 collective-permute-start.6
  13.2 0.1 pad_add_fusion.info_ref
  13.2 0.0 copy-done.2
  13.2 0.0 copy-done.3
  13.2 0.0 copy-done.1
  13.3 1.9 %prep.1 = (bf16[512,256]{1,0:T(8,128)(2,1)S(1)}, s32[8,512]{1,0:T(8,128)S(1)}) custom-call(s32[3]{0:T(128)S(1)} %pad_add_fusion.info_ref, s32[1,512]{1,0:T(1,128)S(1)} %bitcast.17, s32[1,512]{1,0:T(1,128)S(1)} %bitcast.18, bf16[256,512]{1,0:T(8,128)(2,1)S(1)} %bitcast.16), custom_call_target="tpu_custom_call" | custom-call | flops 134217728 | bytes 1048576 | tf_op jit(solution)/shard_map/prep/pallas_call | solution.py:305
  15.1 0.0 collective-permute-done.1.refs_2_
  15.1 1.0 %collective-permute-done.2.refs_3_ = bf16[256,256]{1,0:T(8,128)(2,1)S(1)} collective-permute-done((bf16[256,256]{1,0:T(8,128)(2,1)S(1)}, bf16[256,256]{1,0:T(8,128)(2,1)S(1)}, u32[]{:S(2)}, u32[]{:S(2)}) %collective-permute-start.2) | collective-permute-done | bytes 131104 | tf_op jit(solution)/shard_map/ppermute | solution.py:276
  16.2 0.0 collective-permute-done.4.refs_5_
  16.2 3.2 %collective-permute-done.5.refs_6_ = bf16[256,256]{1,0:T(8,128)(2,1)S(1)} collective-permute-done((bf16[256,256]{1,0:T(8,128)(2,1)S(1)}, bf16[256,256]{1,0:T(8,128)(2,1)S(1)}, u32[]{:S(2)}, u32[]{:S(2)}) %collective-permute-start.5) | collective-permute-done | bytes 131104 | tf_op jit(solution)/shard_map/ppermute | solution.py:276
  19.4 2.9 %collective-permute-done.6.refs_7_ = bf16[256,256]{1,0:T(8,128)(2,1)S(1)} collective-permute-done((bf16[256,256]{1,0:T(8,128)(2,1)S(1)}, bf16[256,256]{1,0:T(8,128)(2,1)S(1)}, u32[]{:S(2)}, u32[]{:S(2)}) %collective-permute-start.6) | collective-permute-done | bytes 131104 | tf_op jit(solution)/shard_map/ppermute | solution.py:276
  22.3 1.4 %blocks_other.1 = (bf16[2064,256]{1,0:T(8,128)(2,1)S(1)}, bf16[2048,256]{1,0:T(8,128)(2,1)S(1)}) custom-call(s32[8,512]{1,0:T(8,128)S(1)} %get-tuple-element.12.table_ref, bf16[512,256]{1,0:T(8,128)(2,1)S(1)} %get-tuple-element.13.ct_ref, bf16[256,256]{1,0:T(8,128)(2,1)S(1)} %get-tuple-element.14.refs_0_, bf16[256,256]{1,0:T(8,128)(2,1)S(1)} %collective-permute-done.refs_1_, ...), custom_call_target="tpu_custom_call" | custom-call | flops 268435456 | bytes 2097152 | tf_op jit(solution)/shard_map/blocks_other/pallas_call | solution.py:323
  23.7 1.3 %collective-permute-start.7 = (bf16[2064,256]{1,0:T(8,128)(2,1)S(1)}, bf16[2064,256]{1,0:T(8,128)(2,1)S(1)}, u32[]{:S(2)}, u32[]{:S(2)}) collective-permute-start(bf16[2064,256]{1,0:T(8,128)(2,1)S(1)} %get-tuple-element.16), channel_id=1, source_target_pairs={{0,1},{1,0},{2,3},{3,2},{4,5},{5,4},{6,7},{7,6},{8,9},{9,8},{10,11... | collective-permute-start | bytes 3170312 | tf_op jit(solution)/shard_map/ppermute | solution.py:276
  25.1 0.1 collective-permute-start.8
  25.2 6.0 %collective-permute-start.9 = (bf16[1024,256]{1,0:T(8,128)(2,1)S(1)}, bf16[1024,256]{1,0:T(8,128)(2,1)S(1)}, u32[]{:S(2)}, u32[]{:S(2)}) collective-permute-start(bf16[1024,256]{1,0:T(8,128)(2,1)S(1)} %get-tuple-element.18), channel_id=1, source_target_pairs={{1,2},{3,4},{5,6},{7,8},{9,10},{11,12},{13,14},{15,16},{17,18},{19... | collective-permute-start | bytes 1572872 | tf_op jit(solution)/shard_map/ppermute | solution.py:292
  31.2 1.4 %blocks_own.1.a_ref = bf16[2064,256]{1,0:T(8,128)(2,1)S(1)} custom-call(s32[8,512]{1,0:T(8,128)S(1)} %get-tuple-element.12.table_ref, bf16[512,256]{1,0:T(8,128)(2,1)S(1)} %get-tuple-element.13.ct_ref, bf16[2048,256]{1,0:T(8,128)(2,1)S(1)} %get-tuple-element.15.refs_0_), custom_call_target="tpu_custom_call" | custom-call | flops 268435456 | bytes 2097152 | tf_op jit(solution)/shard_map/blocks_own/pallas_call | solution.py:325
  32.5 0.0 collective-permute-done.7.b_ref
  32.5 1.1 %pair.1 = bf16[2048,256]{1,0:T(8,128)(2,1)} custom-call(bf16[2064,256]{1,0:T(8,128)(2,1)S(1)} %blocks_own.1.a_ref, bf16[2064,256]{1,0:T(8,128)(2,1)S(1)} %collective-permute-done.7.b_ref), custom_call_target="tpu_custom_call" | custom-call | flops 528384 | bytes 3145728 | tf_op jit(solution)/shard_map/pair/pallas_call | solution.py:326
  33.6 5.4 %all-to-all-start = ((bf16[8,256,256]{2,1,0:T(8,128)(2,1)}), bf16[8,256,256]{2,1,0:T(8,128)(2,1)S(1)}, u32[]{:S(2)}, u32[]{:S(2)}) async-start(bf16[8,256,256]{2,1,0:T(8,128)(2,1)} %bitcast.10), calls=%async_computation | async-start | bytes 2097152 | tf_op jit(solution)/shard_map/all_to_all | solution.py:336
  39.0 0.0 collective-permute-done.8.chip_ref
  39.0 13.7 %collective-permute-done.9.far_ref = bf16[1024,256]{1,0:T(8,128)(2,1)S(1)} collective-permute-done((bf16[1024,256]{1,0:T(8,128)(2,1)S(1)}, bf16[1024,256]{1,0:T(8,128)(2,1)S(1)}, u32[]{:S(2)}, u32[]{:S(2)}) %collective-permute-start.9) | collective-permute-done | bytes 524320 | tf_op jit(solution)/shard_map/ppermute | solution.py:292
  52.7 9.5 %near.1.near_ref = bf16[4096,256]{1,0:T(8,128)(2,1)} custom-call(s32[1]{0:T(128)} %bitcast.2.core_ref, bf16[16,9,256,256]{3,2,1,0:T(8,128)(2,1)} %nb_ref.1, bf16[4096,256]{1,0:T(8,128)(2,1)} %panel_ref.3, bf16[1024,256]{1,0:T(8,128)(2,1)S(1)} %collective-permute-done.8.chip_ref, bf16[1024,256]{1,0:T(8,128)(2,1)S(1)} %collective-permute-done.9.far_ref), custom_call_target="tpu_custom_call" | custom-call | flops 4831838208 | bytes 25165824 | tf_op jit(solution)/shard_map/near/pallas_call | solution.py:358
  62.2 0.0 all-to-all-done.parts
  62.2 3.6 %final.1 = bf16[4096,256]{1,0:T(8,128)(2,1)} custom-call(s32[1]{0:T(128)} %bitcast.place_ref, bf16[8,256,256]{2,1,0:T(8,128)(2,1)S(1)} %all-to-all-done.parts, bf16[16,65536]{1,0:T(8,128)(2,1)} %bitcast.19, bf16[4096,256]{1,0:T(8,128)(2,1)} %near.1.near_ref), custom_call_target="tpu_custom_call" | custom-call | flops 67108864 | bytes 8388608 | tf_op jit(solution)/shard_map/final/pallas_call | solution.py:361
Async XLA Ops:
  0.0 13.2 %copy-start.2 = (s32[1,1,512]{2,1,0:T(1,128)S(1)}, s32[1,1,512]{2,1,0:T(1,128)}, u32[]{:S(2)}) copy-start(s32[1,1,512]{2,1,0:T(1,128)} %param.13) | copy-start | bytes 6148
  0.0 13.2 %copy-start.3 = (s32[1,1,512]{2,1,0:T(1,128)S(1)}, s32[1,1,512]{2,1,0:T(1,128)}, u32[]{:S(2)}) copy-start(s32[1,1,512]{2,1,0:T(1,128)} %param.14) | copy-start | bytes 6148
  0.0 0.9 %copy-start = (bf16[4096,16]{0,1:T(8,128)(2,1)S(1)}, bf16[4096,16]{0,1:T(8,128)(2,1)}, u32[]{:S(2)}) copy-start(bf16[4096,16]{0,1:T(8,128)(2,1)} %param.10) | copy-start | bytes 393220
  0.9 12.3 %copy-start.1 = (bf16[1,1,512,16,16]{2,4,3,1,0:T(8,128)(2,1)S(1)}, bf16[1,1,512,16,16]{2,4,3,1,0:T(8,128)(2,1)}, u32[]{:S(2)}) copy-start(bf16[1,1,512,16,16]{2,4,3,1,0:T(8,128)(2,1)} %param.12) | copy-start | bytes 786436
  3.0 5.6 %collective-permute-start.3 = (bf16[256,256]{1,0:T(8,128)(2,1)S(1)}, bf16[256,256]{1,0:T(8,128)(2,1)S(1)}, u32[]{:S(2)}, u32[]{:S(2)}) collective-permute-start(bf16[256,256]{1,0:T(8,128)(2,1)S(1)} %get-tuple-element.14.refs_0_), channel_id=1, source_target_pairs={{0,64},{64,0},{1,65},{65,1},{2,66},{66,2},{3,67},{67,3},{4,68},{68... | collective-permute-start | bytes 393224 | tf_op jit(solution)/shard_map/ppermute | solution.py:276
  4.7 7.8 %collective-permute-start = (bf16[256,256]{1,0:T(8,128)(2,1)S(1)}, bf16[256,256]{1,0:T(8,128)(2,1)S(1)}, u32[]{:S(2)}, u32[]{:S(2)}) collective-permute-start(bf16[256,256]{1,0:T(8,128)(2,1)S(1)} %get-tuple-element.14.refs_0_), channel_id=1, source_target_pairs={{0,16},{16,0},{32,48},{48,32},{1,17},{17,1},{33,49},{49,33},{2,18}... | collective-permute-start | bytes 393224 | tf_op jit(solution)/shard_map/ppermute | solution.py:276
  6.0 9.1 %collective-permute-start.1 = (bf16[256,256]{1,0:T(8,128)(2,1)S(1)}, bf16[256,256]{1,0:T(8,128)(2,1)S(1)}, u32[]{:S(2)}, u32[]{:S(2)}) collective-permute-start(bf16[256,256]{1,0:T(8,128)(2,1)S(1)} %get-tuple-element.14.refs_0_), channel_id=1, source_target_pairs={{0,32},{16,48},{32,0},{48,16},{1,33},{17,49},{33,1},{49,17},{2,34}... | collective-permute-start | bytes 393224 | tf_op jit(solution)/shard_map/ppermute | solution.py:276
  8.6 7.5 %collective-permute-start.2 = (bf16[256,256]{1,0:T(8,128)(2,1)S(1)}, bf16[256,256]{1,0:T(8,128)(2,1)S(1)}, u32[]{:S(2)}, u32[]{:S(2)}) collective-permute-start(bf16[256,256]{1,0:T(8,128)(2,1)S(1)} %get-tuple-element.14.refs_0_), channel_id=1, source_target_pairs={{0,48},{16,32},{32,16},{48,0},{1,49},{17,33},{33,17},{49,1},{2,50}... | collective-permute-start | bytes 393224 | tf_op jit(solution)/shard_map/ppermute | solution.py:276
  8.6 7.5 %collective-permute-start.4 = (bf16[256,256]{1,0:T(8,128)(2,1)S(1)}, bf16[256,256]{1,0:T(8,128)(2,1)S(1)}, u32[]{:S(2)}, u32[]{:S(2)}) collective-permute-start(bf16[256,256]{1,0:T(8,128)(2,1)S(1)} %collective-permute-done.3.refs_4_), channel_id=1, source_target_pairs={{0,16},{16,0},{32,48},{48,32},{1,17},{17,1},{33,49},{49,33},{2,18}... | collective-permute-start | bytes 393224 | tf_op jit(solution)/shard_map/ppermute | solution.py:276
  9.1 10.3 %collective-permute-start.5 = (bf16[256,256]{1,0:T(8,128)(2,1)S(1)}, bf16[256,256]{1,0:T(8,128)(2,1)S(1)}, u32[]{:S(2)}, u32[]{:S(2)}) collective-permute-start(bf16[256,256]{1,0:T(8,128)(2,1)S(1)} %collective-permute-done.3.refs_4_), channel_id=1, source_target_pairs={{0,32},{16,48},{32,0},{48,16},{1,33},{17,49},{33,1},{49,17},{2,34}... | collective-permute-start | bytes 393224 | tf_op jit(solution)/shard_map/ppermute | solution.py:276
  12.5 9.8 %collective-permute-start.6 = (bf16[256,256]{1,0:T(8,128)(2,1)S(1)}, bf16[256,256]{1,0:T(8,128)(2,1)S(1)}, u32[]{:S(2)}, u32[]{:S(2)}) collective-permute-start(bf16[256,256]{1,0:T(8,128)(2,1)S(1)} %collective-permute-done.3.refs_4_), channel_id=1, source_target_pairs={{0,48},{16,32},{32,16},{48,0},{1,49},{17,33},{33,17},{49,1},{2,50}... | collective-permute-start | bytes 393224 | tf_op jit(solution)/shard_map/ppermute | solution.py:276
  23.7 8.8 %collective-permute-start.7 = (bf16[2064,256]{1,0:T(8,128)(2,1)S(1)}, bf16[2064,256]{1,0:T(8,128)(2,1)S(1)}, u32[]{:S(2)}, u32[]{:S(2)}) collective-permute-start(bf16[2064,256]{1,0:T(8,128)(2,1)S(1)} %get-tuple-element.16), channel_id=1, source_target_pairs={{0,1},{1,0},{2,3},{3,2},{4,5},{5,4},{6,7},{7,6},{8,9},{9,8},{10,11... | collective-permute-start | bytes 3170312 | tf_op jit(solution)/shard_map/ppermute | solution.py:276
  25.1 14.0 %collective-permute-start.8 = (bf16[1024,256]{1,0:T(8,128)(2,1)S(1)}, bf16[1024,256]{1,0:T(8,128)(2,1)S(1)}, u32[]{:S(2)}, u32[]{:S(2)}) collective-permute-start(bf16[1024,256]{1,0:T(8,128)(2,1)S(1)} %get-tuple-element.17), channel_id=1, source_target_pairs={{0,1},{1,0},{2,3},{3,2},{4,5},{5,4},{6,7},{7,6},{8,9},{9,8},{10,11... | collective-permute-start | bytes 1572872 | tf_op jit(solution)/shard_map/ppermute | solution.py:276
  25.2 27.6 %collective-permute-start.9 = (bf16[1024,256]{1,0:T(8,128)(2,1)S(1)}, bf16[1024,256]{1,0:T(8,128)(2,1)S(1)}, u32[]{:S(2)}, u32[]{:S(2)}) collective-permute-start(bf16[1024,256]{1,0:T(8,128)(2,1)S(1)} %get-tuple-element.18), channel_id=1, source_target_pairs={{1,2},{3,4},{5,6},{7,8},{9,10},{11,12},{13,14},{15,16},{17,18},{19... | collective-permute-start | bytes 1572872 | tf_op jit(solution)/shard_map/ppermute | solution.py:292
  33.6 28.6 %all-to-all-start = ((bf16[8,256,256]{2,1,0:T(8,128)(2,1)}), bf16[8,256,256]{2,1,0:T(8,128)(2,1)S(1)}, u32[]{:S(2)}, u32[]{:S(2)}) async-start(bf16[8,256,256]{2,1,0:T(8,128)(2,1)} %bitcast.10), calls=%async_computation | async-start | bytes 2097152 | tf_op jit(solution)/shard_map/all_to_all | solution.py:336

commit v5 on v4

--- a/solution.py
+++ b/solution.py
@@ -57,9 +57,9 @@
         store.wait()
 
 
-def prep_kernel(per_dev, rank, groups, info_ref, rows_ref, cols_ref, x_ref, ct_ref, table_ref):
+def prep_kernel(per_dev, rank, groups, count_ref, core_ref, at_row_ref, rows_ref, cols_ref, x_ref, ct_ref, table_ref):
     slots = rows_ref.shape[1]
-    count, core = info_ref[0], info_ref[1]
+    count, core = count_ref[0, 0], core_ref[0]
     lane = lax.broadcasted_iota(I32, (1, slots), 1)
     live = lane < count
     rows = rows_ref[...]
@@ -87,7 +87,7 @@
     ct_ref[...] = value.astype(BF16)
     top = jnp.max(jnp.where(live, row_key, 0))
     ahead = jnp.sum((live & (row_key < groups // 2)).astype(I32))
-    cols = cols_ref[...] ^ (info_ref[2] * per_dev)
+    cols = cols_ref[...] ^ (at_row_ref[0] * per_dev)
     pair = jnp.concatenate([cols, row_key] + [jnp.zeros_like(row_key)] * 6, axis=0)
     table = lax.dot_general(pair.astype(F32).astype(BF16), pick, NT, preferred_element_type=F32).astype(I32)
     which = lax.broadcasted_iota(I32, table.shape, 0)
@@ -291,18 +291,18 @@
     pairs = [(i, i + 1) for i in range(1, peers - 1, 2)]
     from_far = lax.ppermute(to_far, every, pairs + [(b, a) for a, b in pairs])
 
-    info = jnp.stack([blk_count.reshape(()), core.astype(I32), lax.axis_index(ROW).astype(I32)])
+    at_row = lax.axis_index(ROW).astype(I32).reshape(1)
     x = jnp.transpose(couplings.reshape(slots, rank, rank), (1, 2, 0)).reshape(rank * rank, slots)
     prep = pl.pallas_call(
         functools.partial(prep_kernel, clusters, rank, groups),
         out_shape=(jax.ShapeDtypeStruct((slots, rank * rank), BF16), jax.ShapeDtypeStruct((8, slots), I32)),
-        in_specs=[SMEM, VMEM, VMEM, VMEM],
+        in_specs=[SMEM, SMEM, SMEM, VMEM, VMEM, VMEM],
         out_specs=(VMEM, VMEM),
         compiler_params=params(24),
         cost_estimate=cost(2 * slots * slots * rank * rank, 1 << 20),
         name="prep",
     )
-    ct, table = prep(info, blk_rows.reshape(1, slots), blk_cols.reshape(1, slots), x)
+    ct, table = prep(blk_count, here, at_row, blk_rows.reshape(1, slots), blk_cols.reshape(1, slots), x)
 
     half_rows = groups // 2 * rank
 
@@ -311,7 +311,7 @@
     def blocks(second):
         held_shape = jax.ShapeDtypeStruct((row_peers * clusters * rank, cols), BF16)
         return pl.pallas_call(
-            functools.partial(block_kernel, rank, 128 // rank, 2, second),
+            functools.partial(block_kernel, rank, 128 // rank, 4, second),
             out_shape=kept if second else (kept, held_shape),
             in_specs=[SMEM] + [VMEM] * (2 if second else 1 + row_peers),
             out_specs=VMEM if second else (VMEM, VMEM),
@@ -368,8 +368,8 @@
             pltpu.VMEM((rows, cols), BF16),
             pltpu.VMEM((rows, cols), BF16),
             pltpu.SemaphoreType.DMA,
-            pltpu.SemaphoreType.DMA((chunks,)),
-            pltpu.SemaphoreType.DMA((chunks,)),
+            pltpu.SemaphoreType.DMA((chunks // 2,)),
+            pltpu.SemaphoreType.DMA((chunks // 2,)),
         ],
         compiler_params=params(52),
         cost_estimate=cost(4 * rows * rank * cols, 8 << 20),

time: 66 us -> 65.5 us (level)
  waiting for transfers between devices: 20.8 us -> 21.6 us
where the time goes in v5:
time: 65.5 us; the launch traced here: 65.2 us
  starting transfers between devices  21.8 us (33%)
  waiting for transfers between devices  21.6 us (33%)
  Pallas kernels  20.2 us (31%)
  local copies, waits for them, and re-layouts  0.94 us (1%)
  between operations  0.77 us (1%)
    ppermute x1, waiting for transfers between devices, on_device(): from_far = lax.ppermute(to_far, every, pairs + [(b, a) for a, b in pairs])  13.8 us
    ppermute x9, starting transfers between devices, swap_over(): return lax.ppermute(x, axis, [(i, i ^ bits) for i in range(n)])  10.9 us
    pallas_call x1, Pallas kernels, on_device(): near = near_call(here, near_blocks, panel, from_chip, from_far)  9.49 us
    ppermute x9, waiting for transfers between devices, swap_over(): return lax.ppermute(x, axis, [(i, i ^ bits) for i in range(n)])  7.75 us
    ppermute x1, starting transfers between devices, on_device(): from_far = lax.ppermute(to_far, every, pairs + [(b, a) for a, b in pairs])  5.9 us
    all_to_all x1, starting transfers between devices, on_device(): lax.all_to_all(summed.reshape(col_peers // 2, clusters * rank, cols), ('x...  4.93 us
    pallas_call x1, Pallas kernels, on_device(): pl.pallas_call(functools.partial(final_kernel, rank, leaf), out_shape=jax...  3.17 us
    pallas_call x1, Pallas kernels, on_device(): own, to_chip, to_far = coeffs(here, panel, col_basis.T)  2.06 us
  transfers between devices with their start and end apart: 11, of which 4 were waited for; matrix products, arithmetic and copies ran while one was open for 0% of the time, Pallas kernels for 21%

profile of v5, /device:TPU:5, one launch (start us, length us, event | category | flops | bytes accessed | tf_op | source)
XLA Modules:
  0.0 65.2 jit_solution(2405713183031325854)
XLA Ops:
  0.0 0.0 copy-start.2
  0.0 0.0 copy-start.3
  0.0 0.0 copy-start
  0.0 0.9 %copy-done = bf16[4096,16]{0,1:T(8,128)(2,1)S(1)} copy-done((bf16[4096,16]{0,1:T(8,128)(2,1)S(1)}, bf16[4096,16]{0,1:T(8,128)(2,1)}, u32[]{:S(2)}) %copy-start) | copy-done | bytes 131096
  0.9 0.0 copy-start.1
  0.9 2.1 %coeffs.1 = (bf16[256,256]{1,0:T(8,128)(2,1)S(1)}, bf16[1024,256]{1,0:T(8,128)(2,1)S(1)}, bf16[1024,256]{1,0:T(8,128)(2,1)S(1)}) custom-call(s32[1]{0:T(128)} %bitcast.1.core_ref, bf16[4096,256]{1,0:T(8,128)(2,1)} %panel_ref.3, bf16[16,4096]{1,0:T(8,128)(2,1)S(1)} %bitcast.13), custom_call_target="tpu_custom_call" | custom-call | flops 33554432 | bytes 5242880 | tf_op jit(solution)/shard_map/coeffs/pallas_call | solution.py:272
  3.0 1.7 %collective-permute-start.3 = (bf16[256,256]{1,0:T(8,128)(2,1)S(1)}, bf16[256,256]{1,0:T(8,128)(2,1)S(1)}, u32[]{:S(2)}, u32[]{:S(2)}) collective-permute-start(bf16[256,256]{1,0:T(8,128)(2,1)S(1)} %get-tuple-element.14.refs_0_), channel_id=1, source_target_pairs={{0,64},{64,0},{1,65},{65,1},{2,66},{66,2},{3,67},{67,3},{4,68},{68... | collective-permute-start | bytes 393224 | tf_op jit(solution)/shard_map/ppermute | solution.py:276
  4.7 1.3 %collective-permute-start = (bf16[256,256]{1,0:T(8,128)(2,1)S(1)}, bf16[256,256]{1,0:T(8,128)(2,1)S(1)}, u32[]{:S(2)}, u32[]{:S(2)}) collective-permute-start(bf16[256,256]{1,0:T(8,128)(2,1)S(1)} %get-tuple-element.14.refs_0_), channel_id=1, source_target_pairs={{0,16},{16,0},{32,48},{48,32},{1,17},{17,1},{33,49},{49,33},{2,18}... | collective-permute-start | bytes 393224 | tf_op jit(solution)/shard_map/ppermute | solution.py:276
  6.0 2.6 %collective-permute-start.1 = (bf16[256,256]{1,0:T(8,128)(2,1)S(1)}, bf16[256,256]{1,0:T(8,128)(2,1)S(1)}, u32[]{:S(2)}, u32[]{:S(2)}) collective-permute-start(bf16[256,256]{1,0:T(8,128)(2,1)S(1)} %get-tuple-element.14.refs_0_), channel_id=1, source_target_pairs={{0,32},{16,48},{32,0},{48,16},{1,33},{17,49},{33,1},{49,17},{2,34}... | collective-permute-start | bytes 393224 | tf_op jit(solution)/shard_map/ppermute | solution.py:276
  8.6 0.0 collective-permute-start.2
  8.6 0.0 collective-permute-done.3.refs_4_
  8.6 0.5 collective-permute-start.4
  9.1 3.4 %collective-permute-start.5 = (bf16[256,256]{1,0:T(8,128)(2,1)S(1)}, bf16[256,256]{1,0:T(8,128)(2,1)S(1)}, u32[]{:S(2)}, u32[]{:S(2)}) collective-permute-start(bf16[256,256]{1,0:T(8,128)(2,1)S(1)} %collective-permute-done.3.refs_4_), channel_id=1, source_target_pairs={{0,32},{16,48},{32,0},{48,16},{1,33},{17,49},{33,1},{49,17},{2,34}... | collective-permute-start | bytes 393224 | tf_op jit(solution)/shard_map/ppermute | solution.py:276
  12.5 0.0 collective-permute-done.refs_1_
  12.5 0.0 collective-permute-start.6
  13.2 0.0 copy-done.2
  13.2 0.0 copy-done.3
  13.2 0.0 copy-done.1
  13.2 1.3 %prep.1 = (bf16[512,256]{1,0:T(8,128)(2,1)S(1)}, s32[8,512]{1,0:T(8,128)S(1)}) custom-call(s32[1,1]{1,0:T(1,128)S(6)} %copy.9.count_ref, s32[1]{0:T(128)} %bitcast.1.core_ref, s32[1]{0:T(128)} %bitcast.2.at_row_ref, s32[1,512]{1,0:T(1,128)S(1)} %bitcast.15, s32[1,512]{1,0:T(1,128)S(1)} %bitcast.16, bf16[256,512]{1,0:T(8,128)(2,1)S(1)} %bitcast.14), custom_call_target="tpu_custom_call" | custom-call | flops 134217728 | bytes 1048576 | tf_op jit(solution)/shard_map/prep/pallas_call | solution.py:305
  14.5 0.0 collective-permute-done.1.refs_2_
  14.6 1.6 %collective-permute-done.2.refs_3_ = bf16[256,256]{1,0:T(8,128)(2,1)S(1)} collective-permute-done((bf16[256,256]{1,0:T(8,128)(2,1)S(1)}, bf16[256,256]{1,0:T(8,128)(2,1)S(1)}, u32[]{:S(2)}, u32[]{:S(2)}) %collective-permute-start.2) | collective-permute-done | bytes 131104 | tf_op jit(solution)/shard_map/ppermute | solution.py:276
  16.2 0.0 collective-permute-done.4.refs_5_
  16.2 3.2 %collective-permute-done.5.refs_6_ = bf16[256,256]{1,0:T(8,128)(2,1)S(1)} collective-permute-done((bf16[256,256]{1,0:T(8,128)(2,1)S(1)}, bf16[256,256]{1,0:T(8,128)(2,1)S(1)}, u32[]{:S(2)}, u32[]{:S(2)}) %collective-permute-start.5) | collective-permute-done | bytes 131104 | tf_op jit(solution)/shard_map/ppermute | solution.py:276
  19.4 2.9 %collective-permute-done.6.refs_7_ = bf16[256,256]{1,0:T(8,128)(2,1)S(1)} collective-permute-done((bf16[256,256]{1,0:T(8,128)(2,1)S(1)}, bf16[256,256]{1,0:T(8,128)(2,1)S(1)}, u32[]{:S(2)}, u32[]{:S(2)}) %collective-permute-start.6) | collective-permute-done | bytes 131104 | tf_op jit(solution)/shard_map/ppermute | solution.py:276
  22.3 1.3 %blocks_other.1 = (bf16[2064,256]{1,0:T(8,128)(2,1)S(1)}, bf16[2048,256]{1,0:T(8,128)(2,1)S(1)}) custom-call(s32[8,512]{1,0:T(8,128)S(1)} %get-tuple-element.12.table_ref, bf16[512,256]{1,0:T(8,128)(2,1)S(1)} %get-tuple-element.13.ct_ref, bf16[256,256]{1,0:T(8,128)(2,1)S(1)} %get-tuple-element.14.refs_0_, bf16[256,256]{1,0:T(8,128)(2,1)S(1)} %collective-permute-done.refs_1_, ...), custom_call_target="tpu_custom_call" | custom-call | flops 268435456 | bytes 2097152 | tf_op jit(solution)/shard_map/blocks_other/pallas_call | solution.py:323
  23.6 1.3 %collective-permute-start.7 = (bf16[2064,256]{1,0:T(8,128)(2,1)S(1)}, bf16[2064,256]{1,0:T(8,128)(2,1)S(1)}, u32[]{:S(2)}, u32[]{:S(2)}) collective-permute-start(bf16[2064,256]{1,0:T(8,128)(2,1)S(1)} %get-tuple-element.16), channel_id=1, source_target_pairs={{0,1},{1,0},{2,3},{3,2},{4,5},{5,4},{6,7},{7,6},{8,9},{9,8},{10,11... | collective-permute-start | bytes 3170312 | tf_op jit(solution)/shard_map/ppermute | solution.py:276
  25.0 0.1 collective-permute-start.8
  25.1 5.9 %collective-permute-start.9 = (bf16[1024,256]{1,0:T(8,128)(2,1)S(1)}, bf16[1024,256]{1,0:T(8,128)(2,1)S(1)}, u32[]{:S(2)}, u32[]{:S(2)}) collective-permute-start(bf16[1024,256]{1,0:T(8,128)(2,1)S(1)} %get-tuple-element.18), channel_id=1, source_target_pairs={{1,2},{3,4},{5,6},{7,8},{9,10},{11,12},{13,14},{15,16},{17,18},{19... | collective-permute-start | bytes 1572872 | tf_op jit(solution)/shard_map/ppermute | solution.py:292
  31.0 1.7 %blocks_own.1.a_ref = bf16[2064,256]{1,0:T(8,128)(2,1)S(1)} custom-call(s32[8,512]{1,0:T(8,128)S(1)} %get-tuple-element.12.table_ref, bf16[512,256]{1,0:T(8,128)(2,1)S(1)} %get-tuple-element.13.ct_ref, bf16[2048,256]{1,0:T(8,128)(2,1)S(1)} %get-tuple-element.15.refs_0_), custom_call_target="tpu_custom_call" | custom-call | flops 268435456 | bytes 2097152 | tf_op jit(solution)/shard_map/blocks_own/pallas_call | solution.py:325
  32.7 0.0 collective-permute-done.7.b_ref
  32.7 1.1 %pair.1 = bf16[2048,256]{1,0:T(8,128)(2,1)} custom-call(bf16[2064,256]{1,0:T(8,128)(2,1)S(1)} %blocks_own.1.a_ref, bf16[2064,256]{1,0:T(8,128)(2,1)S(1)} %collective-permute-done.7.b_ref), custom_call_target="tpu_custom_call" | custom-call | flops 528384 | bytes 3145728 | tf_op jit(solution)/shard_map/pair/pallas_call | solution.py:326
  33.8 4.9 %all-to-all-start = ((bf16[8,256,256]{2,1,0:T(8,128)(2,1)}), bf16[8,256,256]{2,1,0:T(8,128)(2,1)S(1)}, u32[]{:S(2)}, u32[]{:S(2)}) async-start(bf16[8,256,256]{2,1,0:T(8,128)(2,1)} %bitcast.9), calls=%async_computation | async-start | bytes 2097152 | tf_op jit(solution)/shard_map/all_to_all | solution.py:336
  38.7 0.0 collective-permute-done.8.chip_ref
  38.7 13.8 %collective-permute-done.9.far_ref = bf16[1024,256]{1,0:T(8,128)(2,1)S(1)} collective-permute-done((bf16[1024,256]{1,0:T(8,128)(2,1)S(1)}, bf16[1024,256]{1,0:T(8,128)(2,1)S(1)}, u32[]{:S(2)}, u32[]{:S(2)}) %collective-permute-start.9) | collective-permute-done | bytes 524320 | tf_op jit(solution)/shard_map/ppermute | solution.py:292
  52.5 9.5 %near.1.near_ref = bf16[4096,256]{1,0:T(8,128)(2,1)} custom-call(s32[1]{0:T(128)} %bitcast.1.core_ref, bf16[16,9,256,256]{3,2,1,0:T(8,128)(2,1)} %nb_ref.1, bf16[4096,256]{1,0:T(8,128)(2,1)} %panel_ref.3, bf16[1024,256]{1,0:T(8,128)(2,1)S(1)} %collective-permute-done.8.chip_ref, bf16[1024,256]{1,0:T(8,128)(2,1)S(1)} %collective-permute-done.9.far_ref), custom_call_target="tpu_custom_call" | custom-call | flops 4831838208 | bytes 25165824 | tf_op jit(solution)/shard_map/near/pallas_call | solution.py:358
  62.0 0.0 all-to-all-done.parts
  62.0 3.2 %final.1 = bf16[4096,256]{1,0:T(8,128)(2,1)} custom-call(s32[1]{0:T(128)} %bitcast.place_ref, bf16[8,256,256]{2,1,0:T(8,128)(2,1)S(1)} %all-to-all-done.parts, bf16[16,65536]{1,0:T(8,128)(2,1)} %bitcast.17, bf16[4096,256]{1,0:T(8,128)(2,1)} %near.1.near_ref), custom_call_target="tpu_custom_call" | custom-call | flops 67108864 | bytes 8388608 | tf_op jit(solution)/shard_map/final/pallas_call | solution.py:361
Async XLA Ops:
  0.0 13.2 %copy-start.2 = (s32[1,1,512]{2,1,0:T(1,128)S(1)}, s32[1,1,512]{2,1,0:T(1,128)}, u32[]{:S(2)}) copy-start(s32[1,1,512]{2,1,0:T(1,128)} %param.13) | copy-start | bytes 6148
  0.0 13.2 %copy-start.3 = (s32[1,1,512]{2,1,0:T(1,128)S(1)}, s32[1,1,512]{2,1,0:T(1,128)}, u32[]{:S(2)}) copy-start(s32[1,1,512]{2,1,0:T(1,128)} %param.14) | copy-start | bytes 6148
  0.0 0.9 %copy-start = (bf16[4096,16]{0,1:T(8,128)(2,1)S(1)}, bf16[4096,16]{0,1:T(8,128)(2,1)}, u32[]{:S(2)}) copy-start(bf16[4096,16]{0,1:T(8,128)(2,1)} %param.10) | copy-start | bytes 393220
  0.9 12.3 %copy-start.1 = (bf16[1,1,512,16,16]{2,4,3,1,0:T(8,128)(2,1)S(1)}, bf16[1,1,512,16,16]{2,4,3,1,0:T(8,128)(2,1)}, u32[]{:S(2)}) copy-start(bf16[1,1,512,16,16]{2,4,3,1,0:T(8,128)(2,1)} %param.12) | copy-start | bytes 786436
  3.0 5.6 %collective-permute-start.3 = (bf16[256,256]{1,0:T(8,128)(2,1)S(1)}, bf16[256,256]{1,0:T(8,128)(2,1)S(1)}, u32[]{:S(2)}, u32[]{:S(2)}) collective-permute-start(bf16[256,256]{1,0:T(8,128)(2,1)S(1)} %get-tuple-element.14.refs_0_), channel_id=1, source_target_pairs={{0,64},{64,0},{1,65},{65,1},{2,66},{66,2},{3,67},{67,3},{4,68},{68... | collective-permute-start | bytes 393224 | tf_op jit(solution)/shard_map/ppermute | solution.py:276
  4.7 7.8 %collective-permute-start = (bf16[256,256]{1,0:T(8,128)(2,1)S(1)}, bf16[256,256]{1,0:T(8,128)(2,1)S(1)}, u32[]{:S(2)}, u32[]{:S(2)}) collective-permute-start(bf16[256,256]{1,0:T(8,128)(2,1)S(1)} %get-tuple-element.14.refs_0_), channel_id=1, source_target_pairs={{0,16},{16,0},{32,48},{48,32},{1,17},{17,1},{33,49},{49,33},{2,18}... | collective-permute-start | bytes 393224 | tf_op jit(solution)/shard_map/ppermute | solution.py:276
  6.0 8.5 %collective-permute-start.1 = (bf16[256,256]{1,0:T(8,128)(2,1)S(1)}, bf16[256,256]{1,0:T(8,128)(2,1)S(1)}, u32[]{:S(2)}, u32[]{:S(2)}) collective-permute-start(bf16[256,256]{1,0:T(8,128)(2,1)S(1)} %get-tuple-element.14.refs_0_), channel_id=1, source_target_pairs={{0,32},{16,48},{32,0},{48,16},{1,33},{17,49},{33,1},{49,17},{2,34}... | collective-permute-start | bytes 393224 | tf_op jit(solution)/shard_map/ppermute | solution.py:276
  8.6 7.5 %collective-permute-start.2 = (bf16[256,256]{1,0:T(8,128)(2,1)S(1)}, bf16[256,256]{1,0:T(8,128)(2,1)S(1)}, u32[]{:S(2)}, u32[]{:S(2)}) collective-permute-start(bf16[256,256]{1,0:T(8,128)(2,1)S(1)} %get-tuple-element.14.refs_0_), channel_id=1, source_target_pairs={{0,48},{16,32},{32,16},{48,0},{1,49},{17,33},{33,17},{49,1},{2,50}... | collective-permute-start | bytes 393224 | tf_op jit(solution)/shard_map/ppermute | solution.py:276
  8.6 7.5 %collective-permute-start.4 = (bf16[256,256]{1,0:T(8,128)(2,1)S(1)}, bf16[256,256]{1,0:T(8,128)(2,1)S(1)}, u32[]{:S(2)}, u32[]{:S(2)}) collective-permute-start(bf16[256,256]{1,0:T(8,128)(2,1)S(1)} %collective-permute-done.3.refs_4_), channel_id=1, source_target_pairs={{0,16},{16,0},{32,48},{48,32},{1,17},{17,1},{33,49},{49,33},{2,18}... | collective-permute-start | bytes 393224 | tf_op jit(solution)/shard_map/ppermute | solution.py:276
  9.1 10.3 %collective-permute-start.5 = (bf16[256,256]{1,0:T(8,128)(2,1)S(1)}, bf16[256,256]{1,0:T(8,128)(2,1)S(1)}, u32[]{:S(2)}, u32[]{:S(2)}) collective-permute-start(bf16[256,256]{1,0:T(8,128)(2,1)S(1)} %collective-permute-done.3.refs_4_), channel_id=1, source_target_pairs={{0,32},{16,48},{32,0},{48,16},{1,33},{17,49},{33,1},{49,17},{2,34}... | collective-permute-start | bytes 393224 | tf_op jit(solution)/shard_map/ppermute | solution.py:276
  12.5 9.8 %collective-permute-start.6 = (bf16[256,256]{1,0:T(8,128)(2,1)S(1)}, bf16[256,256]{1,0:T(8,128)(2,1)S(1)}, u32[]{:S(2)}, u32[]{:S(2)}) collective-permute-start(bf16[256,256]{1,0:T(8,128)(2,1)S(1)} %collective-permute-done.3.refs_4_), channel_id=1, source_target_pairs={{0,48},{16,32},{32,16},{48,0},{1,49},{17,33},{33,17},{49,1},{2,50}... | collective-permute-start | bytes 393224 | tf_op jit(solution)/shard_map/ppermute | solution.py:276
  23.6 9.1 %collective-permute-start.7 = (bf16[2064,256]{1,0:T(8,128)(2,1)S(1)}, bf16[2064,256]{1,0:T(8,128)(2,1)S(1)}, u32[]{:S(2)}, u32[]{:S(2)}) collective-permute-start(bf16[2064,256]{1,0:T(8,128)(2,1)S(1)} %get-tuple-element.16), channel_id=1, source_target_pairs={{0,1},{1,0},{2,3},{3,2},{4,5},{5,4},{6,7},{7,6},{8,9},{9,8},{10,11... | collective-permute-start | bytes 3170312 | tf_op jit(solution)/shard_map/ppermute | solution.py:276
  25.0 13.7 %collective-permute-start.8 = (bf16[1024,256]{1,0:T(8,128)(2,1)S(1)}, bf16[1024,256]{1,0:T(8,128)(2,1)S(1)}, u32[]{:S(2)}, u32[]{:S(2)}) collective-permute-start(bf16[1024,256]{1,0:T(8,128)(2,1)S(1)} %get-tuple-element.17), channel_id=1, source_target_pairs={{0,1},{1,0},{2,3},{3,2},{4,5},{5,4},{6,7},{7,6},{8,9},{9,8},{10,11... | collective-permute-start | bytes 1572872 | tf_op jit(solution)/shard_map/ppermute | solution.py:276
  25.1 27.5 %collective-permute-start.9 = (bf16[1024,256]{1,0:T(8,128)(2,1)S(1)}, bf16[1024,256]{1,0:T(8,128)(2,1)S(1)}, u32[]{:S(2)}, u32[]{:S(2)}) collective-permute-start(bf16[1024,256]{1,0:T(8,128)(2,1)S(1)} %get-tuple-element.18), channel_id=1, source_target_pairs={{1,2},{3,4},{5,6},{7,8},{9,10},{11,12},{13,14},{15,16},{17,18},{19... | collective-permute-start | bytes 1572872 | tf_op jit(solution)/shard_map/ppermute | solution.py:292
  33.8 28.3 %all-to-all-start = ((bf16[8,256,256]{2,1,0:T(8,128)(2,1)}), bf16[8,256,256]{2,1,0:T(8,128)(2,1)S(1)}, u32[]{:S(2)}, u32[]{:S(2)}) async-start(bf16[8,256,256]{2,1,0:T(8,128)(2,1)} %bitcast.9), calls=%async_computation | async-start | bytes 2097152 | tf_op jit(solution)/shard_map/all_to_all | solution.py:336
